TPU v7x, 128 devices: a whole 4x4x4 slice. The times are simulated.
128 devices in a mesh: out: 8 (over x, y_lo), con: 16 (over z, y_hi, core).
Axes of the slice: x: 4, y: 4 (y_hi: 2, y_lo: 2; y = y_hi * 2 + y_lo), z: 4, core: 2. Of those that a mesh axis runs over, the one named last changes fastest.
Arguments:
- fitted_factors: bfloat16 [512, 512, 1536], P('out', 'con'), may hold values from -0.119628906 to 0.119628906
- amplitudes: bfloat16 [512, 512, 256], P(None, 'con'), may hold values from -1.796875 to 1.796875
- driver_term: float32 [4, 256, 512], P(None, None, 'out'), may hold values from -9 to 9
- occ_energy: float32 [16], replicated, may hold values from -1 to -0.5
- vir_energy: float32 [512], replicated, may hold values from 0.5 to 1.5
- window_rows: int32 [4], replicated, may hold values from 0 to 511, as said below
Outputs:
- first_update: bfloat16 [4, 256, 512], P(None, 'con', 'out')
- second_update: bfloat16 [4, 256, 512], P(None, 'con', 'out')
Inputs may be any that keep to these rules, and one draw needn't show every extreme that they name: `window_rows`: the 4 entries are distinct.
All inputs are finite; a program needn't handle non-finite values.
Results may differ from a plain program's by a relative error of at most 0.006.
Values may be sent and summed in bfloat16 or wider, within the bound.
No kernel may reach another device: no remote copies, remote signals or barrier semaphores. Data moves between devices by JAX's collectives and lax.ppermute only.
A program may use at most 128 MiB of HBM per device.

v0:
```python
import jax
import jax.numpy as jnp
from jax import lax
from jax.experimental import pallas as pl
from jax.experimental.pallas import tpu as pltpu
from jax.sharding import Mesh, PartitionSpec as P


OUT = ("x", "yl")
CON = ("z", "yh", "core")
CHIPS = ("x", "yl", "z", "yh")
FINE = (4, 2, 4, 2, 2)
D_STEP = 8
f32, bf16 = jnp.float32, jnp.bfloat16


def copy_for_each(value, axis):
    size = lax.axis_size(axis)
    return lax.all_to_all(
        jnp.broadcast_to(value[None], (size, *value.shape)), axis, 0, 0, tiled=True
    )


def swap_cores(value):
    return lax.ppermute(value, "core", [(0, 1), (1, 0)])


def dot_t(a, b):
    return lax.dot_general(a, b, (((1,), (1,)), ((), ())), preferred_element_type=f32)


def select_rows(local, factors):
    window = local.shape[0]
    block_b, block_d, aux = factors.shape

    def body(local_ref, f_ref, o_ref):
        row = local_ref[pl.program_id(0)]
        mine = (row >= 0) & (row < block_b)
        o_ref[...] = jnp.where(mine, f_ref[...], jnp.zeros_like(f_ref))

    def row_map(k, local_ref):
        return (jnp.clip(local_ref[k], 0, block_b - 1), 0, 0)

    return pl.pallas_call(
        body,
        grid_spec=pltpu.PrefetchScalarGridSpec(
            num_scalar_prefetch=1,
            grid=(window,),
            in_specs=[pl.BlockSpec((1, block_d, aux), row_map)],
            out_specs=pl.BlockSpec((1, block_d, aux), lambda k, _: (k, 0, 0)),
        ),
        out_shape=jax.ShapeDtypeStruct((window, block_d, aux), bf16),
        name="select_rows",
    )(local, factors)


def window_dots(vectors, factors):
    n, aux = vectors.shape
    block_d, block_b, _ = factors.shape

    def body(v_ref, f_ref, o_ref):
        o_ref[...] = dot_t(v_ref[...], f_ref[...].reshape(-1, aux)).astype(bf16)

    return pl.pallas_call(
        body,
        grid=(block_d // D_STEP,),
        in_specs=[
            pl.BlockSpec((n, aux), lambda i: (0, 0)),
            pl.BlockSpec((D_STEP, block_b, aux), lambda i: (i, 0, 0)),
        ],
        out_specs=pl.BlockSpec((n, D_STEP * block_b), lambda i: (0, i)),
        out_shape=jax.ShapeDtypeStruct((n, block_d * block_b), bf16),
        name="window_dots",
    )(vectors, factors)


def ladder_sums(core, rows, f_own, f_other, t_all, t_other, window):
    count, aux = rows.shape
    block_d, block_b, _ = f_own.shape
    _, _, c_half, pairs = t_all.shape
    steps = block_d // D_STEP

    def body(core_ref, a_ref, f1_ref, f2_ref, t1_ref, t2_ref, o_ref, lhs_ref, acc_ref):
        i = pl.program_id(0)

        @pl.when(i == 0)
        def _():
            acc_ref[...] = jnp.zeros_like(acc_ref)

        def step(f, t):
            for k in range(window):
                p = dot_t(f, a_ref[k * c_half : (k + 1) * c_half, :]).astype(bf16)
                for d in range(D_STEP):
                    lhs_ref[k * block_b : (k + 1) * block_b, d * c_half : (d + 1) * c_half] = p[
                        d * block_b : (d + 1) * block_b, :
                    ]
            acc_ref[...] += jnp.dot(lhs_ref[...], t, preferred_element_type=f32)

        @pl.when(i < steps)
        def _():
            step(f1_ref[...].reshape(-1, aux), t1_ref[...].reshape(-1, pairs))

        @pl.when(i >= steps)
        def _():
            step(f2_ref[...].reshape(-1, aux), t2_ref[...].reshape(-1, pairs))

        @pl.when(i == 2 * steps - 1)
        def _():
            o_ref[...] = acc_ref[...].T

    def first(i):
        return jnp.minimum(i, steps - 1)

    def second(i):
        return jnp.maximum(i - steps, 0)

    flops = 2 * 2 * block_d * block_b * count * (aux + pairs)
    return pl.pallas_call(
        body,
        grid_spec=pltpu.PrefetchScalarGridSpec(
            num_scalar_prefetch=1,
            grid=(2 * steps,),
            in_specs=[
                pl.BlockSpec((count, aux), lambda i, c: (0, 0)),
                pl.BlockSpec((D_STEP, block_b, aux), lambda i, c: (first(i), 0, 0)),
                pl.BlockSpec((D_STEP, block_b, aux), lambda i, c: (second(i), 0, 0)),
                pl.BlockSpec((1, D_STEP, c_half, pairs), lambda i, c: (c[0], first(i), 0, 0)),
                pl.BlockSpec((D_STEP, c_half, pairs), lambda i, c: (second(i), 0, 0)),
            ],
            out_specs=pl.BlockSpec((pairs, window * block_b), lambda i, c: (0, 0)),
            scratch_shapes=[
                pltpu.VMEM((window * block_b, D_STEP * c_half), bf16),
                pltpu.VMEM((window * block_b, pairs), f32),
            ],
        ),
        out_shape=jax.ShapeDtypeStruct((pairs, window * block_b), f32),
        cost_estimate=pl.CostEstimate(flops=flops, bytes_accessed=24_000_000, transcendentals=0),
        name="ladder_sums",
    )(core, rows, f_own, f_other, t_all, t_other)


def first_step(tiles, driver, denom, window):
    _, own_pairs, width = tiles.shape
    block_b = width // window

    def body(t_ref, d_ref, e_ref, l_ref, w_ref, o_ref):
        ladder = jnp.sum(t_ref[...], axis=0)
        l_ref[...] = ladder
        value = ((d_ref[...] + ladder) / e_ref[...]).astype(bf16)
        w_ref[...] = value
        for k in range(window):
            o_ref[k] = value[:, k * block_b : (k + 1) * block_b]

    return pl.pallas_call(
        body,
        out_shape=(
            jax.ShapeDtypeStruct((own_pairs, width), f32),
            jax.ShapeDtypeStruct((own_pairs, width), bf16),
            jax.ShapeDtypeStruct((window, own_pairs, block_b), bf16),
        ),
        name="first_step",
    )(tiles, driver, denom)


def second_step(first_all, old, blocks, ladder, driver, denom, window):
    outs, own_pairs, width = first_all.shape
    cons = blocks.shape[0]
    block_b = width // window
    per = cons // outs
    block_d = block_b // per

    def body(f_ref, p_ref, w_ref, l_ref, d_ref, e_ref, o_ref, s_ref):
        total = l_ref[...]
        for o in range(outs):
            delta = (f_ref[o].astype(f32) - p_ref[o].astype(f32)).astype(bf16)
            for m in range(window):
                for h in range(per):
                    at = m * block_b + h * block_d
                    s_ref[at : at + block_d, :] = w_ref[
                        per * o + h, m * block_d : (m + 1) * block_d, :
                    ]
            total = total + jnp.dot(delta, s_ref[...], preferred_element_type=f32)
        value = ((d_ref[...] + total) / e_ref[...]).astype(bf16)
        for k in range(window):
            o_ref[k] = value[:, k * block_b : (k + 1) * block_b]

    return pl.pallas_call(
        body,
        out_shape=jax.ShapeDtypeStruct((window, own_pairs, block_b), bf16),
        scratch_shapes=[pltpu.VMEM((width, width), bf16)],
        name="second_step",
    )(first_all, old, blocks, ladder, driver, denom)


def update(fitted_factors, amplitudes, driver_term, occ_energy, vir_energy, window_rows):
    block_b, block_d, aux = fitted_factors.shape
    virtuals, _, pairs = amplitudes.shape
    window = window_rows.shape[0]
    out_index = lax.axis_index(OUT)
    con_index = lax.axis_index(CON)
    core = lax.axis_index("core").astype(jnp.int32)
    outs, cons = lax.axis_size(OUT), lax.axis_size(CON)
    groups = cons // 2
    half = window * block_d // outs
    parts = block_d // half
    c_half = parts * groups * half
    own_pairs = pairs // cons

    owned = select_rows(window_rows - out_index.astype(jnp.int32) * block_b, fitted_factors)
    tiles = lax.all_to_all(owned.reshape(outs, half, aux), OUT, 0, 0, tiled=True)
    piece = jnp.sum(tiles.astype(f32), axis=0).astype(bf16)
    piece, factors = lax.optimization_barrier((piece, fitted_factors))
    piece, amplitudes = lax.optimization_barrier((piece, amplitudes))
    rows = copy_for_each(piece, CHIPS)
    rows = rows.reshape(window * c_half, aux)

    f_own = factors.transpose(1, 0, 2)
    f_other = swap_cores(f_own)
    t_all = amplitudes.reshape(groups, 2, parts, half, block_d, pairs)
    t_all = t_all.transpose(1, 4, 2, 0, 3, 5).reshape(2, block_d, c_half, pairs)
    t_other = swap_cores(lax.dynamic_index_in_dim(t_all, 1 - core, 0, False))

    part_i = jnp.arange(parts)[:, None, None]
    group_i = jnp.arange(groups)[None, :, None]
    r_i = jnp.arange(half)[None, None, :]
    c_index = ((group_i * 2 + core) * block_d + part_i * half + r_i).reshape(-1)

    old = jnp.concatenate(
        [lax.dynamic_slice_in_dim(amplitudes, window_rows[m], 1, 0) for m in range(window)]
    )
    width = window * block_b
    old = old.reshape(window, block_d, cons, own_pairs).transpose(2, 3, 0, 1)
    old = old.reshape(cons, -1, width)

    mask = window_rows[:, None] == jnp.arange(virtuals, dtype=jnp.int32)[None, :]
    window_energy = jnp.sum(jnp.where(mask, vir_energy[None, :], 0.0), axis=1)
    local_energy = lax.dynamic_slice_in_dim(vir_energy, out_index * block_b, block_b, 0)
    pair_energy = (occ_energy[:, None] + occ_energy[None, :]).reshape(-1)
    pair_energy = lax.dynamic_slice_in_dim(pair_energy, con_index * own_pairs, own_pairs, 0)
    denom = (window_energy[:, None] + local_energy[None, :]).reshape(1, -1) - pair_energy[:, None]
    driver = lax.dynamic_slice_in_dim(driver_term, con_index * own_pairs, own_pairs, 1)
    driver = driver.transpose(1, 0, 2).reshape(own_pairs, width)

    rows, f_own, f_other, t_all, t_other, old, denom, driver = lax.optimization_barrier(
        (rows, f_own, f_other, t_all, t_other, old, denom, driver)
    )

    at_window = (window_rows[:, None] == c_index[None, :]).astype(bf16)
    vectors = jnp.einsum(
        "mc,kcq->mkq", at_window, rows.reshape(window, c_half, aux), preferred_element_type=f32
    ).astype(bf16)
    vectors = vectors.reshape(window * window, aux)
    vectors = vectors + swap_cores(vectors)
    blocks = window_dots(vectors, f_own)
    blocks = blocks.reshape(window, window, block_d, block_b).transpose(0, 2, 1, 3)
    blocks = blocks.reshape(window * block_d, width)
    sent = jnp.concatenate(
        [jnp.broadcast_to(blocks[None], (cons, *blocks.shape)), old], axis=1
    )
    sent, rows = lax.optimization_barrier((sent, rows))
    got = lax.all_to_all(sent, CON, 0, 0, tiled=True)

    ladder = ladder_sums(core[None], rows, f_own, f_other, t_all, t_other, window)
    ladder, got = lax.optimization_barrier((ladder, got))
    tiles = lax.all_to_all(ladder.reshape(cons, own_pairs, width), CON, 0, 0, tiled=True)
    ladder_own, first_wide, first_own = first_step(tiles, driver, denom, window)
    first_all = copy_for_each(first_wide, OUT)

    old_all = got[:, window * block_d :].reshape(outs, cons // outs, own_pairs, window, block_d)
    old_all = old_all.transpose(0, 2, 3, 1, 4).reshape(outs, own_pairs, width)
    second_own = second_step(first_all, old_all, got, ladder_own, driver, denom, window)
    return (first_own, second_own)


def solution(mesh):
    fine = Mesh(mesh.devices.reshape(FINE), OUT + CON)
    return jax.shard_map(
        update,
        mesh=fine,
        in_specs=(P(OUT, CON, None), P(None, CON, None), P(None, None, OUT), P(), P(), P()),
        out_specs=(P(None, CON, OUT), P(None, CON, OUT)),
        check_vma=False,
    )
```

profile of v0, /device:TPU:1, one launch (start us, length us, event | category | flops | bytes accessed | tf_op | source)
XLA Modules:
  0.0 170.4 jit_solution(15238069319024149405)
XLA Ops:
  0.6 0.0 copy-start
  0.7 1.2 broadcast_subtract_fusion.1.local_ref
  1.9 2.9 %select_rows.1 = bf16[4,32,1536]{2,1,0:T(8,128)(2,1)} custom-call(s32[4]{0:T(128)} %broadcast_subtract_fusion.1.local_ref, bf16[64,32,1536]{2,1,0:T(8,128)(2,1)} %f_ref.1), custom_call_target="tpu_custom_call" | custom-call | tf_op jit(solution)/shard_map/select_rows/pallas_call | solution.py:44
  4.8 14.0 %all_to_all.25 = bf16[8,16,1536]{2,1,0:T(8,128)(2,1)S(1)} all-to-all(bf16[8,16,1536]{2,1,0:T(8,128)(2,1)} %bitcast.35), channel_id=1, replica_groups=mesh['x'=4,'yl'=2,'z'=4,'yh'=2,'core'=2] {'x','yl'}, dimensions={0} | all-to-all | bytes 786432 | tf_op jit(solution)/shard_map/all_to_all | solution.py:210
  18.8 0.1 reduce_sum.21
  18.8 8.9 %copy.44 = bf16[64,32,1536]{2,0,1:T(8,128)(2,1)} copy(bf16[64,32,1536]{2,1,0:T(8,128)(2,1)} %f_ref.1) | data formatting | bytes 12582912 | tf_op jit(solution)/shard_map/optimization_barrier | solution.py:212
  27.8 2.2 %collective-permute-start = (bf16[32,64,1536]{2,1,0:T(8,128)(2,1)}, bf16[32,64,1536]{2,1,0:T(8,128)(2,1)}, u32[]{:S(2)}, u32[]{:S(2)}) collective-permute-start(bf16[32,64,1536]{2,1,0:T(8,128)(2,1)} %bitcast.29.f_ref.f1_ref), channel_id=1, source_target_pairs={{0,1},{1,0},{2,3},{3,2},{4,5},{5,4},{6,7},{7,6},{8,9},{9,8},{10,11... | collective-permute-start | bytes 18874376 | tf_op jit(solution)/shard_map/ppermute | solution.py:25
  29.9 11.4 %copy.35 = bf16[8,2,2,16,32,256]{5,3,0,2,4,1:T(8,128)(2,1)} copy(bf16[8,2,2,16,32,256]{5,4,3,2,1,0:T(8,128)(2,1)} %bitcast.34) | data formatting | bytes 16777216 | tf_op jit(solution)/shard_map/reshape | solution.py:219
  41.3 4.6 %dynamic-slice_bitcast_fusion = bf16[32,256,256]{2,1,0:T(8,128)(2,1)} fusion(bf16[2,32,256,256]{3,2,1,0:T(8,128)(2,1)} %bitcast.30, s32[]{:T(128)S(6)} %select_n.27), kind=kLoop, calls=%fused_computation.1 | loop fusion | bytes 8388612 | tf_op jit(solution)/shard_map/jit(dynamic_index_in_dim)/squeeze | solution.py:221
  45.9 0.0 collective-permute-start.1
  45.9 2.0 %broadcast_in_dim.23 = bf16[64,16,1536]{2,1,0:T(8,128)(2,1)} broadcast(bf16[16,1536]{1,0:T(8,128)(2,1)S(1)} %reduce_sum.21), dimensions={1,2} | broadcast | bytes 3194880 | tf_op jit(solution)/shard_map/broadcast_in_dim | solution.py:20
  47.9 0.0 copy-start.4
  47.9 0.0 copy-start.5
  47.9 9.6 %all-to-all-start.1 = ((bf16[64,16,1536]{2,1,0:T(8,128)(2,1)}), bf16[64,16,1536]{2,1,0:T(8,128)(2,1)S(1)}, u32[]{:S(2)}, u32[]{:S(2)}) async-start(bf16[64,16,1536]{2,1,0:T(8,128)(2,1)} %broadcast_in_dim.23), calls=%async_computation.1 | async-start | bytes 6291456 | tf_op jit(solution)/shard_map/all_to_all | solution.py:19
  57.5 0.0 copy-done.4
  57.6 0.6 fusion.4
  63.0 0.0 copy-done.5
  63.0 0.1 broadcast_add_fusion
  63.0 0.1 add.145
  63.1 0.0 copy-done.6
  63.1 0.1 dynamic_slice.30
  63.2 0.2 select_reduce_fusion
  63.4 0.1 broadcast_add_fusion.1
  63.5 0.1 add.141
  63.5 0.1 dynamic_slice.31
  63.6 0.0 copy-done
  63.6 0.1 constant_dynamic-slice_fusion
  63.7 0.7 copy.42.d_ref
  64.4 0.1 broadcast_add_fusion.2
  64.5 0.1 iota_add_fusion
  64.6 0.1 add.130
  67.1 0.7 broadcast_subtract_fusion.e_ref
  67.7 0.8 constant_dynamic-slice_fusion.4
  68.5 0.9 copy.36
  69.4 1.8 %copy.37 = bf16[16,16,4,32]{3,2,1,0:T(4,128)(2,1)} copy(bf16[16,16,4,32]{3,1,0,2:T(8,128)(2,1)} %bitcast.36) | data formatting | bytes 131072 | tf_op jit(solution)/shard_map/transpose | solution.py:232
  71.2 1.8 %reshape.137 = bf16[16,8,256]{2,1,0:T(8,128)(2,1)} reshape(bf16[16,16,4,32]{3,2,1,0:T(4,128)(2,1)} %copy.37) | data formatting | bytes 131072 | tf_op jit(solution)/shard_map/reshape | solution.py:233
  73.0 24.3 %all-to-all-done.1 = bf16[64,16,1536]{2,1,0:T(8,128)(2,1)S(1)} async-done(((bf16[64,16,1536]{2,1,0:T(8,128)(2,1)}), bf16[64,16,1536]{2,1,0:T(8,128)(2,1)S(1)}, u32[]{:S(2)}, u32[]{:S(2)}) %all-to-all-start.1) | async-done | bytes 3145760 | tf_op jit(solution)/shard_map/all_to_all | solution.py:19
  97.3 0.0 collective-permute-done.1.t2_ref
  97.3 0.0 collective-permute-done.f2_ref
  97.3 0.6 convolution_convert_fusion
  98.0 2.3 %collective-permute-start.2 = (bf16[16,1536]{1,0:T(8,128)(2,1)S(1)}, bf16[16,1536]{1,0:T(8,128)(2,1)S(1)}, u32[]{:S(2)}, u32[]{:S(2)}) collective-permute-start(bf16[16,1536]{1,0:T(8,128)(2,1)S(1)} %reshape.140), channel_id=1, source_target_pairs={{0,1},{1,0},{2,3},{3,2},{4,5},{5,4},{6,7},{7,6},{8,9},{9,8},{10,11... | collective-permute-start | bytes 147464 | tf_op jit(solution)/shard_map/ppermute | solution.py:25
  100.2 0.9 collective-permute-done.2
  101.1 0.6 add.149.v_ref
  101.7 5.2 %window_dots.1 = bf16[16,2048]{1,0:T(8,128)(2,1)} custom-call(bf16[16,1536]{1,0:T(8,128)(2,1)} %add.149.v_ref, bf16[32,64,1536]{2,1,0:T(8,128)(2,1)} %bitcast.29.f_ref.f1_ref), custom_call_target="tpu_custom_call" | custom-call | tf_op jit(solution)/shard_map/window_dots/pallas_call | solution.py:64
  106.9 0.0 copy-done.1
  106.9 1.0 reshape.141
  107.9 0.1 copy.40
  108.0 0.1 broadcast_in_dim.26
  108.2 0.1 broadcast_in_dim.27
  108.3 2.0 %pad_maximum_fusion = bf16[16,136,256]{2,1,0:T(8,128)(2,1)} fusion(bf16[16,8,256]{2,1,0:T(8,128)(2,1)} %reshape.137, bf16[16,128,256]{2,1,0:T(8,128)(2,1)S(1)} %broadcast_in_dim.27), kind=kLoop, calls=%fused_computation.3 | loop fusion | flops 2228224 | bytes 2228224 | tf_op jit(solution)/shard_map/concatenate | solution.py:257
  110.3 3.8 %all-to-all-start.2 = ((bf16[16,136,256]{2,1,0:T(8,128)(2,1)}), bf16[16,136,256]{2,1,0:T(8,128)(2,1)S(1)}, u32[]{:S(2)}, u32[]{:S(2)}) async-start(bf16[16,136,256]{2,1,0:T(8,128)(2,1)} %pad_maximum_fusion), calls=%async_computation.2 | async-start | bytes 2228224 | tf_op jit(solution)/shard_map/all_to_all | solution.py:261
  114.1 25.4 %ladder_sums.1 = f32[256,256]{1,0:T(8,128)} custom-call(s32[1]{0:T(128)} %bitcast.core_ref, bf16[1024,1536]{1,0:T(8,128)(2,1)} %bitcast.33, bf16[32,64,1536]{2,1,0:T(8,128)(2,1)} %bitcast.29.f_ref.f1_ref, bf16[32,64,1536]{2,1,0:T(8,128)(2,1)} %collective-permute-done.f2_ref, bf16[2,32,256,256]{3,2,1,0:T(8,128)(2,1)} %bitcast.31, ...), custom_call_target="tpu_custom_call" | custom-call | flops 15032385536 | bytes 24000000 | tf_op jit(solution)/shard_map/ladder_sums/pallas_call | solution.py:118
  139.5 0.0 all-to-all-done.2.w_ref
  139.5 16.1 %all_to_all.26.t_ref = f32[16,16,256]{2,1,0:T(8,128)} all-to-all(f32[16,16,256]{2,1,0:T(8,128)} %bitcast.40), channel_id=1, replica_groups=mesh['x'=4,'yl'=2,'z'=4,'yh'=2,'core'=2] {'z','yh','core'}, dimensions={0} | all-to-all | bytes 524288 | tf_op jit(solution)/shard_map/all_to_all | solution.py:265
  155.6 1.7 first_step.1
  157.2 1.3 broadcast_in_dim.28
  158.6 3.8 %all-to-all-start.4 = ((bf16[8,16,256]{2,1,0:T(8,128)(2,1)}), bf16[8,16,256]{2,1,0:T(8,128)(2,1)S(1)}, u32[]{:S(2)}, u32[]{:S(2)}) async-start(bf16[8,16,256]{2,1,0:T(8,128)(2,1)} %broadcast_in_dim.28), calls=%async_computation.4 | async-start | bytes 131072 | tf_op jit(solution)/shard_map/all_to_all | solution.py:19
  162.4 0.2 reshape.143
  162.6 0.4 copy.41
  163.0 0.8 reshape.144.p_ref
  163.8 3.7 %all-to-all-done.4.f_ref = bf16[8,16,256]{2,1,0:T(8,128)(2,1)S(1)} async-done(((bf16[8,16,256]{2,1,0:T(8,128)(2,1)}), bf16[8,16,256]{2,1,0:T(8,128)(2,1)S(1)}, u32[]{:S(2)}, u32[]{:S(2)}) %all-to-all-start.4) | async-done | bytes 65568 | tf_op jit(solution)/shard_map/all_to_all | solution.py:19
  167.5 0.0 copy-done.2
  167.5 0.6 copy-done.3
  168.1 2.3 %second_step.1 = bf16[4,16,64]{2,1,0:T(8,128)(2,1)} custom-call(bf16[8,16,256]{2,1,0:T(8,128)(2,1)} %copy-done.3, bf16[8,16,256]{2,1,0:T(8,128)(2,1)} %reshape.144.p_ref, bf16[16,136,256]{2,1,0:T(8,128)(2,1)} %copy-done.2, f32[16,256]{1,0:T(8,128)} %get-tuple-element.39.l_ref, f32[16,256]{1,0:T(8,128)} %copy.42.d_ref, f32[16,256]{1,0:T(8,128)} %broadcast_subtract_fusion.e_ref), custom_call_target="tpu_custom_call" | custom-call | tf_op jit(solution)/shard_map/second_step/pallas_call | solution.py:187
  (10 shorter events, 0.1 us)
Async XLA Ops:
  0.6 63.0 %copy-start = (f32[4,256,64]{1,2,0:T(8,128)S(1)}, f32[4,256,64]{1,2,0:T(8,128)}, u32[]{:S(2)}) copy-start(f32[4,256,64]{1,2,0:T(8,128)} %param.8) | copy-start | bytes 786436
  27.8 69.6 %collective-permute-start = (bf16[32,64,1536]{2,1,0:T(8,128)(2,1)}, bf16[32,64,1536]{2,1,0:T(8,128)(2,1)}, u32[]{:S(2)}, u32[]{:S(2)}) collective-permute-start(bf16[32,64,1536]{2,1,0:T(8,128)(2,1)} %bitcast.29.f_ref.f1_ref), channel_id=1, source_target_pairs={{0,1},{1,0},{2,3},{3,2},{4,5},{5,4},{6,7},{7,6},{8,9},{9,8},{10,11... | collective-permute-start | bytes 18874376 | tf_op jit(solution)/shard_map/ppermute | solution.py:25
  45.9 51.4 %collective-permute-start.1 = (bf16[32,256,256]{2,1,0:T(8,128)(2,1)}, bf16[32,256,256]{2,1,0:T(8,128)(2,1)}, u32[]{:S(2)}, u32[]{:S(2)}) collective-permute-start(bf16[32,256,256]{2,1,0:T(8,128)(2,1)} %dynamic-slice_bitcast_fusion), channel_id=1, source_target_pairs={{0,1},{1,0},{2,3},{3,2},{4,5},{5,4},{6,7},{7,6},{8,9},{9,8},{10,11... | collective-permute-start | bytes 12582920 | tf_op jit(solution)/shard_map/ppermute | solution.py:25
  47.9 9.6 %copy-start.4 = (s32[4]{0:T(128)S(1)}, s32[4]{0:T(128)}, u32[]{:S(2)}) copy-start(s32[4]{0:T(128)} %param.11) | copy-start | bytes 52
  47.9 15.0 %copy-start.5 = (f32[16]{0:T(128)S(1)}, f32[16]{0:T(128)}, u32[]{:S(2)}) copy-start(f32[16]{0:T(128)} %param.9) | copy-start | bytes 196
  47.9 15.2 %copy-start.6 = (f32[512]{0:T(512)S(1)}, f32[512]{0:T(512)}, u32[]{:S(2)}) copy-start(f32[512]{0:T(512)} %param.10) | copy-start | bytes 6148
  47.9 49.4 %all-to-all-start.1 = ((bf16[64,16,1536]{2,1,0:T(8,128)(2,1)}), bf16[64,16,1536]{2,1,0:T(8,128)(2,1)S(1)}, u32[]{:S(2)}, u32[]{:S(2)}) async-start(bf16[64,16,1536]{2,1,0:T(8,128)(2,1)} %broadcast_in_dim.23), calls=%async_computation.1 | async-start | bytes 6291456 | tf_op jit(solution)/shard_map/all_to_all | solution.py:19
  97.3 9.6 %copy-start.1 = (bf16[64,16,1536]{2,1,0:T(8,128)(2,1)}, bf16[64,16,1536]{2,1,0:T(8,128)(2,1)S(1)}, u32[]{:S(2)}) copy-start(bf16[64,16,1536]{2,1,0:T(8,128)(2,1)S(1)} %all-to-all-done.1) | copy-start | bytes 9437188
  98.0 3.1 %collective-permute-start.2 = (bf16[16,1536]{1,0:T(8,128)(2,1)S(1)}, bf16[16,1536]{1,0:T(8,128)(2,1)S(1)}, u32[]{:S(2)}, u32[]{:S(2)}) collective-permute-start(bf16[16,1536]{1,0:T(8,128)(2,1)S(1)} %reshape.140), channel_id=1, source_target_pairs={{0,1},{1,0},{2,3},{3,2},{4,5},{5,4},{6,7},{7,6},{8,9},{9,8},{10,11... | collective-permute-start | bytes 147464 | tf_op jit(solution)/shard_map/ppermute | solution.py:25
  110.3 29.2 %all-to-all-start.2 = ((bf16[16,136,256]{2,1,0:T(8,128)(2,1)}), bf16[16,136,256]{2,1,0:T(8,128)(2,1)S(1)}, u32[]{:S(2)}, u32[]{:S(2)}) async-start(bf16[16,136,256]{2,1,0:T(8,128)(2,1)} %pad_maximum_fusion), calls=%async_computation.2 | async-start | bytes 2228224 | tf_op jit(solution)/shard_map/all_to_all | solution.py:261
  139.5 28.0 %copy-start.2 = (bf16[16,136,256]{2,1,0:T(8,128)(2,1)}, bf16[16,136,256]{2,1,0:T(8,128)(2,1)S(1)}, u32[]{:S(2)}) copy-start(bf16[16,136,256]{2,1,0:T(8,128)(2,1)S(1)} %all-to-all-done.2.w_ref) | copy-start | bytes 3342340
  158.6 8.9 %all-to-all-start.4 = ((bf16[8,16,256]{2,1,0:T(8,128)(2,1)}), bf16[8,16,256]{2,1,0:T(8,128)(2,1)S(1)}, u32[]{:S(2)}, u32[]{:S(2)}) async-start(bf16[8,16,256]{2,1,0:T(8,128)(2,1)} %broadcast_in_dim.28), calls=%async_computation.4 | async-start | bytes 131072 | tf_op jit(solution)/shard_map/all_to_all | solution.py:19
  167.5 0.6 copy-start.3
where the time goes:
time: 173 us; the launch traced here: 170 us
  local copies, waits for them, and re-layouts  38.8 us (22%)
  Pallas kernels  37.4 us (22%)
  blocking collectives  30.1 us (17%)
  waiting for transfers between devices  28.9 us (17%)
  starting transfers between devices  21.7 us (13%)
  between operations  7.98 us (5%)
  other arithmetic  5.05 us (3%)
    all_to_all x2, waiting for transfers between devices, copy_for_each(): lax.all_to_all(jnp.broadcast_to(value[None], (size, *value.shape)), axis,...  28 us
    pallas_call x1, Pallas kernels, ladder_sums(): pl.pallas_call(body, grid_spec=pltpu.PrefetchScalarGridSpec(num_scalar_pr...  25.4 us
    all_to_all x1, blocking collectives, update(): lax.all_to_all(ladder.reshape(cons, own_pairs, width), CON, 0, 0, tiled=T...  16.1 us
    all_to_all x1, blocking collectives, update(): lax.all_to_all(owned.reshape(outs, half, aux), OUT, 0, 0, tiled=True)  14 us
    all_to_all x2, starting transfers between devices, copy_for_each(): lax.all_to_all(jnp.broadcast_to(value[None], (size, *value.shape)), axis,...  13.4 us
    reshape x1, local copies, waits for them, and re-layouts, update(): t_all = amplitudes.reshape(groups, 2, parts, half, block_d, pairs)  11.4 us
    optimization_barrier x1, local copies, waits for them, and re-layouts, update(): piece, factors = lax.optimization_barrier((piece, fitted_factors))  8.94 us
    pallas_call x1, Pallas kernels, window_dots(): pl.pallas_call(body, grid=(block_d // D_STEP,), in_specs=[pl.BlockSpec((n...  5.18 us
  transfers between devices with their start and end apart: 6, of which 3 were waited for; matrix products, arithmetic and copies ran while one was open for 16% of the time, Pallas kernels for 15%

commit v1 on v0

--- a/solution.py
+++ b/solution.py
@@ -54,24 +54,58 @@
     )(local, factors)
 
 
-def window_dots(vectors, factors):
+def window_blocks(vectors, more, factors, old):
     n, aux = vectors.shape
     block_d, block_b, _ = factors.shape
-
-    def body(v_ref, f_ref, o_ref):
-        o_ref[...] = dot_t(v_ref[...], f_ref[...].reshape(-1, aux)).astype(bf16)
-
-    return pl.pallas_call(
-        body,
-        grid=(block_d // D_STEP,),
+    cons, tail, width = old.shape
+    window = width // block_b
+    steps = block_d // D_STEP
+    count = window * block_d
+
+    def body(v_ref, u_ref, f_ref, p_ref, o_ref, w_ref):
+        v = v_ref[...] + u_ref[...]
+        v = jnp.concatenate([v, jnp.zeros((128 - n, aux), v.dtype)])
+        x = dot_t(f_ref[...].reshape(-1, aux), v).T[:n]
+        i = pl.program_id(0)
+        for s in range(steps):
+
+            @pl.when(i == s)
+            def _():
+                for d in range(D_STEP):
+                    y = x[:, d * block_b : (d + 1) * block_b]
+                    for h in range(width // 128):
+                        w_ref[pl.ds(h * count + s * D_STEP + d, window, stride=block_d), :] = (
+                            jnp.concatenate(
+                                [
+                                    y[k * window : (k + 1) * window]
+                                    for k in range(h * 128 // block_b, (h + 1) * 128 // block_b)
+                                ],
+                                axis=1,
+                            )
+                        )
+
+        @pl.when(i == steps - 1)
+        def _():
+            for h in range(width // 128):
+                w = w_ref[h * count : (h + 1) * count].astype(bf16)
+                for j in range(cons):
+                    o_ref[j, :count, h * 128 : (h + 1) * 128] = w
+            o_ref[:, count:] = p_ref[...]
+
+    return pl.pallas_call(
+        body,
+        grid=(steps,),
         in_specs=[
             pl.BlockSpec((n, aux), lambda i: (0, 0)),
+            pl.BlockSpec((n, aux), lambda i: (0, 0)),
             pl.BlockSpec((D_STEP, block_b, aux), lambda i: (i, 0, 0)),
+            pl.BlockSpec(old.shape, lambda i: (0, 0, 0)),
         ],
-        out_specs=pl.BlockSpec((n, D_STEP * block_b), lambda i: (0, i)),
-        out_shape=jax.ShapeDtypeStruct((n, block_d * block_b), bf16),
-        name="window_dots",
-    )(vectors, factors)
+        out_specs=pl.BlockSpec((cons, count + tail, width), lambda i: (0, 0, 0)),
+        out_shape=jax.ShapeDtypeStruct((cons, count + tail, width), bf16),
+        scratch_shapes=[pltpu.VMEM((width // 128 * count, 128), f32)],
+        name="window_blocks",
+    )(vectors, more, factors, old)
 
 
 def ladder_sums(core, rows, f_own, f_other, t_all, t_other, window):
@@ -139,7 +173,7 @@
     )(core, rows, f_own, f_other, t_all, t_other)
 
 
-def first_step(tiles, driver, denom, window):
+def first_step(tiles, driver, denom, window, outs):
     _, own_pairs, width = tiles.shape
     block_b = width // window
 
@@ -147,7 +181,8 @@
         ladder = jnp.sum(t_ref[...], axis=0)
         l_ref[...] = ladder
         value = ((d_ref[...] + ladder) / e_ref[...]).astype(bf16)
-        w_ref[...] = value
+        for o in range(outs):
+            w_ref[o] = value
         for k in range(window):
             o_ref[k] = value[:, k * block_b : (k + 1) * block_b]
 
@@ -155,7 +190,7 @@
         body,
         out_shape=(
             jax.ShapeDtypeStruct((own_pairs, width), f32),
-            jax.ShapeDtypeStruct((own_pairs, width), bf16),
+            jax.ShapeDtypeStruct((outs, own_pairs, width), bf16),
             jax.ShapeDtypeStruct((window, own_pairs, block_b), bf16),
         ),
         name="first_step",
@@ -247,24 +282,18 @@
 
     at_window = (window_rows[:, None] == c_index[None, :]).astype(bf16)
     vectors = jnp.einsum(
-        "mc,kcq->mkq", at_window, rows.reshape(window, c_half, aux), preferred_element_type=f32
+        "mc,kcq->kmq", at_window, rows.reshape(window, c_half, aux), preferred_element_type=f32
     ).astype(bf16)
     vectors = vectors.reshape(window * window, aux)
-    vectors = vectors + swap_cores(vectors)
-    blocks = window_dots(vectors, f_own)
-    blocks = blocks.reshape(window, window, block_d, block_b).transpose(0, 2, 1, 3)
-    blocks = blocks.reshape(window * block_d, width)
-    sent = jnp.concatenate(
-        [jnp.broadcast_to(blocks[None], (cons, *blocks.shape)), old], axis=1
-    )
+    sent = window_blocks(vectors, swap_cores(vectors), f_own, old)
     sent, rows = lax.optimization_barrier((sent, rows))
     got = lax.all_to_all(sent, CON, 0, 0, tiled=True)
 
     ladder = ladder_sums(core[None], rows, f_own, f_other, t_all, t_other, window)
     ladder, got = lax.optimization_barrier((ladder, got))
     tiles = lax.all_to_all(ladder.reshape(cons, own_pairs, width), CON, 0, 0, tiled=True)
-    ladder_own, first_wide, first_own = first_step(tiles, driver, denom, window)
-    first_all = copy_for_each(first_wide, OUT)
+    ladder_own, first_wide, first_own = first_step(tiles, driver, denom, window, outs)
+    first_all = lax.all_to_all(first_wide, OUT, 0, 0, tiled=True)
 
     old_all = got[:, window * block_d :].reshape(outs, cons // outs, own_pairs, window, block_d)
     old_all = old_all.transpose(0, 2, 3, 1, 4).reshape(outs, own_pairs, width)

time: 173 us -> 169 us (0.977)
  other arithmetic: 5.05 us -> 2.43 us
  local copies, waits for them, and re-layouts: 38.8 us -> 36.7 us
    all_to_all x2 -> x1, waiting for transfers between devices: 28 us -> 24 us  [copy_for_each(): lax.all_to_all(jnp.broadcast_to(value[None], (size, *value.shape)), axis,...]
    all_to_all x2 -> x1, starting transfers between devices: 13.4 us -> 9.46 us  [copy_for_each(): lax.all_to_all(jnp.broadcast_to(value[None], (size, *value.shape)), axis,...]
    all_to_all x0 -> x1, starting transfers between devices: none -> 3.79 us  [update(): first_all = lax.all_to_all(first_wide, OUT, 0, 0, tiled=True)]
    all_to_all x0 -> x1, waiting for transfers between devices: none -> 3.69 us  [update(): first_all = lax.all_to_all(first_wide, OUT, 0, 0, tiled=True)]
    concatenate x1 -> x0, other arithmetic: 1.99 us -> none  [update(): jnp.concatenate([jnp.broadcast_to(blocks[None], (cons, *blocks.shape)), o...]
  transfers between devices with their start and end apart: 6 -> 6, of which waited for: 3 -> 3; matrix products, arithmetic and copies ran while one was open for 16% -> 17% of each run, Pallas kernels for 15% -> 15%
where the time goes in v1:
time: 169 us; the launch traced here: 167 us
  Pallas kernels  38.4 us (23%)
  local copies, waits for them, and re-layouts  36.7 us (22%)
  blocking collectives  30.1 us (18%)
  waiting for transfers between devices  28.5 us (17%)
  starting transfers between devices  21.5 us (13%)
  between operations  8.28 us (5%)
  other arithmetic  2.43 us (1%)
    pallas_call x1, Pallas kernels, ladder_sums(): pl.pallas_call(body, grid_spec=pltpu.PrefetchScalarGridSpec(num_scalar_pr...  25.4 us
    all_to_all x1, waiting for transfers between devices, copy_for_each(): lax.all_to_all(jnp.broadcast_to(value[None], (size, *value.shape)), axis,...  24 us
    all_to_all x1, blocking collectives, update(): lax.all_to_all(ladder.reshape(cons, own_pairs, width), CON, 0, 0, tiled=T...  16.1 us
    all_to_all x1, blocking collectives, update(): lax.all_to_all(owned.reshape(outs, half, aux), OUT, 0, 0, tiled=True)  14 us
    reshape x1, local copies, waits for them, and re-layouts, update(): t_all = amplitudes.reshape(groups, 2, parts, half, block_d, pairs)  11.4 us
    all_to_all x1, starting transfers between devices, copy_for_each(): lax.all_to_all(jnp.broadcast_to(value[None], (size, *value.shape)), axis,...  9.46 us
    optimization_barrier x1, local copies, waits for them, and re-layouts, update(): piece, factors = lax.optimization_barrier((piece, fitted_factors))  8.95 us
    pallas_call x1, Pallas kernels, window_blocks(): pl.pallas_call(body, grid=(steps,), in_specs=[pl.BlockSpec((n, aux), lamb...  6.14 us
  transfers between devices with their start and end apart: 6, of which 3 were waited for; matrix products, arithmetic and copies ran while one was open for 17% of the time, Pallas kernels for 15%

profile of v1, /device:TPU:1, one launch (start us, length us, event | category | flops | bytes accessed | tf_op | source)
XLA Modules:
  0.0 166.5 jit_solution(1588215584614883730)
XLA Ops:
  0.6 0.0 copy-start
  0.7 1.2 broadcast_subtract_fusion.1.local_ref
  1.9 2.9 %select_rows.1 = bf16[4,32,1536]{2,1,0:T(8,128)(2,1)} custom-call(s32[4]{0:T(128)} %broadcast_subtract_fusion.1.local_ref, bf16[64,32,1536]{2,1,0:T(8,128)(2,1)} %f_ref.1), custom_call_target="tpu_custom_call" | custom-call | tf_op jit(solution)/shard_map/select_rows/pallas_call | solution.py:44
  4.8 14.0 %all_to_all.25 = bf16[8,16,1536]{2,1,0:T(8,128)(2,1)S(1)} all-to-all(bf16[8,16,1536]{2,1,0:T(8,128)(2,1)} %bitcast.36), channel_id=1, replica_groups=mesh['x'=4,'yl'=2,'z'=4,'yh'=2,'core'=2] {'x','yl'}, dimensions={0} | all-to-all | bytes 786432 | tf_op jit(solution)/shard_map/all_to_all | solution.py:245
  18.8 0.1 reduce_sum.21
  18.8 8.9 %copy.36 = bf16[64,32,1536]{2,0,1:T(8,128)(2,1)} copy(bf16[64,32,1536]{2,1,0:T(8,128)(2,1)} %f_ref.1) | data formatting | bytes 12582912 | tf_op jit(solution)/shard_map/optimization_barrier | solution.py:247
  27.8 2.2 %collective-permute-start = (bf16[32,64,1536]{2,1,0:T(8,128)(2,1)}, bf16[32,64,1536]{2,1,0:T(8,128)(2,1)}, u32[]{:S(2)}, u32[]{:S(2)}) collective-permute-start(bf16[32,64,1536]{2,1,0:T(8,128)(2,1)} %bitcast.30.f_ref.f1_ref), channel_id=1, source_target_pairs={{0,1},{1,0},{2,3},{3,2},{4,5},{5,4},{6,7},{7,6},{8,9},{9,8},{10,11... | collective-permute-start | bytes 18874376 | tf_op jit(solution)/shard_map/ppermute | solution.py:25
  29.9 11.4 %copy.29 = bf16[8,2,2,16,32,256]{5,3,0,2,4,1:T(8,128)(2,1)} copy(bf16[8,2,2,16,32,256]{5,4,3,2,1,0:T(8,128)(2,1)} %bitcast.35) | data formatting | bytes 16777216 | tf_op jit(solution)/shard_map/reshape | solution.py:254
  41.3 4.6 %dynamic-slice_bitcast_fusion = bf16[32,256,256]{2,1,0:T(8,128)(2,1)} fusion(bf16[2,32,256,256]{3,2,1,0:T(8,128)(2,1)} %bitcast.31, s32[]{:T(128)S(6)} %select_n.27), kind=kLoop, calls=%fused_computation.1 | loop fusion | bytes 8388612 | tf_op jit(solution)/shard_map/jit(dynamic_index_in_dim)/squeeze | solution.py:256
  45.9 0.0 copy-start.6
  45.9 0.0 copy-start.7
  45.9 0.0 copy-start.8
  45.9 0.0 collective-permute-start.1
  45.9 2.0 %broadcast_in_dim.13 = bf16[64,16,1536]{2,1,0:T(8,128)(2,1)} broadcast(bf16[16,1536]{1,0:T(8,128)(2,1)S(1)} %reduce_sum.21), dimensions={1,2} | broadcast | bytes 3194880 | tf_op jit(solution)/shard_map/broadcast_in_dim | solution.py:20
  48.0 9.5 %all-to-all-start.1 = ((bf16[64,16,1536]{2,1,0:T(8,128)(2,1)}), bf16[64,16,1536]{2,1,0:T(8,128)(2,1)S(1)}, u32[]{:S(2)}, u32[]{:S(2)}) async-start(bf16[64,16,1536]{2,1,0:T(8,128)(2,1)} %broadcast_in_dim.13), calls=%async_computation.1 | async-start | bytes 6291456 | tf_op jit(solution)/shard_map/all_to_all | solution.py:19
  57.4 0.0 copy-done.6
  57.4 0.6 fusion.5
  63.1 0.0 copy-done.7
  63.1 0.1 broadcast_add_fusion
  63.2 0.1 add.133
  63.3 0.0 copy-done.8
  63.3 0.1 dynamic_slice.30
  63.3 0.2 select_reduce_fusion
  63.5 0.1 broadcast_add_fusion.1
  63.6 0.1 add.129
  63.7 0.1 dynamic_slice.31
  63.8 0.0 copy-done
  63.8 0.1 constant_dynamic-slice_fusion
  63.9 0.7 copy.34.d_ref
  64.6 0.1 broadcast_add_fusion.2
  64.6 0.1 iota_add_fusion
  64.7 0.1 add.145
  67.3 0.7 broadcast_subtract_fusion.e_ref
  68.0 0.8 constant_dynamic-slice_fusion.4
  68.8 0.8 copy.30
  69.6 1.9 %copy.31 = bf16[16,16,4,32]{3,2,1,0:T(4,128)(2,1)} copy(bf16[16,16,4,32]{3,1,0,2:T(8,128)(2,1)} %bitcast.37) | data formatting | bytes 131072 | tf_op jit(solution)/shard_map/transpose | solution.py:267
  71.5 1.8 %reshape.132.p_ref = bf16[16,8,256]{2,1,0:T(8,128)(2,1)} reshape(bf16[16,16,4,32]{3,2,1,0:T(4,128)(2,1)} %copy.31) | data formatting | bytes 131072 | tf_op jit(solution)/shard_map/reshape | solution.py:268
  73.3 24.0 %all-to-all-done.1 = bf16[64,16,1536]{2,1,0:T(8,128)(2,1)S(1)} async-done(((bf16[64,16,1536]{2,1,0:T(8,128)(2,1)}), bf16[64,16,1536]{2,1,0:T(8,128)(2,1)S(1)}, u32[]{:S(2)}, u32[]{:S(2)}) %all-to-all-start.1) | async-done | bytes 3145760 | tf_op jit(solution)/shard_map/all_to_all | solution.py:19
  97.2 0.0 copy-start.1
  97.2 0.0 collective-permute-done.1.t2_ref
  97.2 0.0 collective-permute-done.f2_ref
  97.2 0.6 fusion
  97.8 0.0 copy-start.4
  97.8 2.3 %collective-permute-start.2 = (bf16[16,1536]{1,0:T(8,128)(2,1)S(1)}, bf16[16,1536]{1,0:T(8,128)(2,1)S(1)}, u32[]{:S(2)}, u32[]{:S(2)}) collective-permute-start(bf16[16,1536]{1,0:T(8,128)(2,1)S(1)} %reshape.135.v_ref), channel_id=1, source_target_pairs={{0,1},{1,0},{2,3},{3,2},{4,5},{5,4},{6,7},{7,6},{8,9},{9,8},{10,11... | collective-permute-start | bytes 147464 | tf_op jit(solution)/shard_map/ppermute | solution.py:25
  100.1 0.9 collective-permute-done.2.u_ref
  101.0 0.0 copy-done.4
  101.0 0.0 copy-start.5
  101.0 0.6 copy-done.5
  101.6 6.1 %window_blocks.1 = bf16[16,136,256]{2,1,0:T(8,128)(2,1)} custom-call(bf16[16,1536]{1,0:T(8,128)(2,1)} %copy-done.4, bf16[16,1536]{1,0:T(8,128)(2,1)} %copy-done.5, bf16[32,64,1536]{2,1,0:T(8,128)(2,1)} %bitcast.30.f_ref.f1_ref, bf16[16,8,256]{2,1,0:T(8,128)(2,1)} %reshape.132.p_ref), custom_call_target="tpu_custom_call" | custom-call | tf_op jit(solution)/shard_map/window_blocks/pallas_call | solution.py:95
  107.7 0.0 copy-done.1
  107.7 3.8 %all-to-all-start.2 = ((bf16[16,136,256]{2,1,0:T(8,128)(2,1)}), bf16[16,136,256]{2,1,0:T(8,128)(2,1)S(1)}, u32[]{:S(2)}, u32[]{:S(2)}) async-start(bf16[16,136,256]{2,1,0:T(8,128)(2,1)} %window_blocks.1), calls=%async_computation.2 | async-start | bytes 2228224 | tf_op jit(solution)/shard_map/all_to_all | solution.py:290
  111.5 25.4 %ladder_sums.1 = f32[256,256]{1,0:T(8,128)} custom-call(s32[1]{0:T(128)} %bitcast.core_ref, bf16[1024,1536]{1,0:T(8,128)(2,1)} %bitcast.34, bf16[32,64,1536]{2,1,0:T(8,128)(2,1)} %bitcast.30.f_ref.f1_ref, bf16[32,64,1536]{2,1,0:T(8,128)(2,1)} %collective-permute-done.f2_ref, bf16[2,32,256,256]{3,2,1,0:T(8,128)(2,1)} %bitcast.32, ...), custom_call_target="tpu_custom_call" | custom-call | flops 15032385536 | bytes 24000000 | tf_op jit(solution)/shard_map/ladder_sums/pallas_call | solution.py:152
  136.9 0.0 all-to-all-done.2.w_ref
  136.9 0.0 copy-start.2
  136.9 16.1 %all_to_all.26.t_ref = f32[16,16,256]{2,1,0:T(8,128)} all-to-all(f32[16,16,256]{2,1,0:T(8,128)} %bitcast.40), channel_id=1, replica_groups=mesh['x'=4,'yl'=2,'z'=4,'yh'=2,'core'=2] {'z','yh','core'}, dimensions={0} | all-to-all | bytes 524288 | tf_op jit(solution)/shard_map/all_to_all | solution.py:294
  153.0 1.7 %first_step.1 = (f32[16,256]{1,0:T(8,128)}, bf16[8,16,256]{2,1,0:T(8,128)(2,1)}, bf16[4,16,64]{2,1,0:T(8,128)(2,1)}) custom-call(f32[16,16,256]{2,1,0:T(8,128)} %all_to_all.26.t_ref, f32[16,256]{1,0:T(8,128)} %copy.34.d_ref, f32[16,256]{1,0:T(8,128)} %broadcast_subtract_fusion.e_ref), custom_call_target="tpu_custom_call" | custom-call | tf_op jit(solution)/shard_map/first_step/pallas_call | solution.py:189
  154.7 3.8 %all-to-all-start.4 = ((bf16[8,16,256]{2,1,0:T(8,128)(2,1)}), bf16[8,16,256]{2,1,0:T(8,128)(2,1)S(1)}, u32[]{:S(2)}, u32[]{:S(2)}) async-start(bf16[8,16,256]{2,1,0:T(8,128)(2,1)} %get-tuple-element.37), calls=%async_computation.4 | async-start | bytes 131072 | tf_op jit(solution)/shard_map/all_to_all | solution.py:296
  158.5 0.2 reshape.137
  158.7 0.4 copy.33
  159.1 0.8 reshape.138.p_ref
  159.9 3.7 %all-to-all-done.4.f_ref = bf16[8,16,256]{2,1,0:T(8,128)(2,1)S(1)} async-done(((bf16[8,16,256]{2,1,0:T(8,128)(2,1)}), bf16[8,16,256]{2,1,0:T(8,128)(2,1)S(1)}, u32[]{:S(2)}, u32[]{:S(2)}) %all-to-all-start.4) | async-done | bytes 65568 | tf_op jit(solution)/shard_map/all_to_all | solution.py:296
  163.6 0.0 copy-done.2
  163.6 0.6 copy-done.3
  164.2 2.3 %second_step.1 = bf16[4,16,64]{2,1,0:T(8,128)(2,1)} custom-call(bf16[8,16,256]{2,1,0:T(8,128)(2,1)} %copy-done.3, bf16[8,16,256]{2,1,0:T(8,128)(2,1)} %reshape.138.p_ref, bf16[16,136,256]{2,1,0:T(8,128)(2,1)} %copy-done.2, f32[16,256]{1,0:T(8,128)} %get-tuple-element.39.l_ref, f32[16,256]{1,0:T(8,128)} %copy.34.d_ref, f32[16,256]{1,0:T(8,128)} %broadcast_subtract_fusion.e_ref), custom_call_target="tpu_custom_call" | custom-call | tf_op jit(solution)/shard_map/second_step/pallas_call | solution.py:222
  (6 shorter events, 0.0 us)
Async XLA Ops:
  0.6 63.1 %copy-start = (f32[4,256,64]{1,2,0:T(8,128)S(1)}, f32[4,256,64]{1,2,0:T(8,128)}, u32[]{:S(2)}) copy-start(f32[4,256,64]{1,2,0:T(8,128)} %param.8) | copy-start | bytes 786436
  27.8 69.4 %collective-permute-start = (bf16[32,64,1536]{2,1,0:T(8,128)(2,1)}, bf16[32,64,1536]{2,1,0:T(8,128)(2,1)}, u32[]{:S(2)}, u32[]{:S(2)}) collective-permute-start(bf16[32,64,1536]{2,1,0:T(8,128)(2,1)} %bitcast.30.f_ref.f1_ref), channel_id=1, source_target_pairs={{0,1},{1,0},{2,3},{3,2},{4,5},{5,4},{6,7},{7,6},{8,9},{9,8},{10,11... | collective-permute-start | bytes 18874376 | tf_op jit(solution)/shard_map/ppermute | solution.py:25
  45.9 11.5 %copy-start.6 = (s32[4]{0:T(128)S(1)}, s32[4]{0:T(128)}, u32[]{:S(2)}) copy-start(s32[4]{0:T(128)} %param.11) | copy-start | bytes 52
  45.9 17.2 %copy-start.7 = (f32[16]{0:T(128)S(1)}, f32[16]{0:T(128)}, u32[]{:S(2)}) copy-start(f32[16]{0:T(128)} %param.9) | copy-start | bytes 196
  45.9 17.4 %copy-start.8 = (f32[512]{0:T(512)S(1)}, f32[512]{0:T(512)}, u32[]{:S(2)}) copy-start(f32[512]{0:T(512)} %param.10) | copy-start | bytes 6148
  45.9 51.3 %collective-permute-start.1 = (bf16[32,256,256]{2,1,0:T(8,128)(2,1)}, bf16[32,256,256]{2,1,0:T(8,128)(2,1)}, u32[]{:S(2)}, u32[]{:S(2)}) collective-permute-start(bf16[32,256,256]{2,1,0:T(8,128)(2,1)} %dynamic-slice_bitcast_fusion), channel_id=1, source_target_pairs={{0,1},{1,0},{2,3},{3,2},{4,5},{5,4},{6,7},{7,6},{8,9},{9,8},{10,11... | collective-permute-start | bytes 12582920 | tf_op jit(solution)/shard_map/ppermute | solution.py:25
  48.0 49.2 %all-to-all-start.1 = ((bf16[64,16,1536]{2,1,0:T(8,128)(2,1)}), bf16[64,16,1536]{2,1,0:T(8,128)(2,1)S(1)}, u32[]{:S(2)}, u32[]{:S(2)}) async-start(bf16[64,16,1536]{2,1,0:T(8,128)(2,1)} %broadcast_in_dim.13), calls=%async_computation.1 | async-start | bytes 6291456 | tf_op jit(solution)/shard_map/all_to_all | solution.py:19
  97.2 10.5 %copy-start.1 = (bf16[64,16,1536]{2,1,0:T(8,128)(2,1)}, bf16[64,16,1536]{2,1,0:T(8,128)(2,1)S(1)}, u32[]{:S(2)}) copy-start(bf16[64,16,1536]{2,1,0:T(8,128)(2,1)S(1)} %all-to-all-done.1) | copy-start | bytes 9437188
  97.8 3.1 %copy-start.4 = (bf16[16,1536]{1,0:T(8,128)(2,1)}, bf16[16,1536]{1,0:T(8,128)(2,1)S(1)}, u32[]{:S(2)}) copy-start(bf16[16,1536]{1,0:T(8,128)(2,1)S(1)} %reshape.135.v_ref) | copy-start | bytes 147460
  97.8 3.1 %collective-permute-start.2 = (bf16[16,1536]{1,0:T(8,128)(2,1)S(1)}, bf16[16,1536]{1,0:T(8,128)(2,1)S(1)}, u32[]{:S(2)}, u32[]{:S(2)}) collective-permute-start(bf16[16,1536]{1,0:T(8,128)(2,1)S(1)} %reshape.135.v_ref), channel_id=1, source_target_pairs={{0,1},{1,0},{2,3},{3,2},{4,5},{5,4},{6,7},{7,6},{8,9},{9,8},{10,11... | collective-permute-start | bytes 147464 | tf_op jit(solution)/shard_map/ppermute | solution.py:25
  101.0 0.6 copy-start.5
  107.7 29.2 %all-to-all-start.2 = ((bf16[16,136,256]{2,1,0:T(8,128)(2,1)}), bf16[16,136,256]{2,1,0:T(8,128)(2,1)S(1)}, u32[]{:S(2)}, u32[]{:S(2)}) async-start(bf16[16,136,256]{2,1,0:T(8,128)(2,1)} %window_blocks.1), calls=%async_computation.2 | async-start | bytes 2228224 | tf_op jit(solution)/shard_map/all_to_all | solution.py:290
  136.9 26.7 %copy-start.2 = (bf16[16,136,256]{2,1,0:T(8,128)(2,1)}, bf16[16,136,256]{2,1,0:T(8,128)(2,1)S(1)}, u32[]{:S(2)}) copy-start(bf16[16,136,256]{2,1,0:T(8,128)(2,1)S(1)} %all-to-all-done.2.w_ref) | copy-start | bytes 3342340
  154.7 8.9 %all-to-all-start.4 = ((bf16[8,16,256]{2,1,0:T(8,128)(2,1)}), bf16[8,16,256]{2,1,0:T(8,128)(2,1)S(1)}, u32[]{:S(2)}, u32[]{:S(2)}) async-start(bf16[8,16,256]{2,1,0:T(8,128)(2,1)} %get-tuple-element.37), calls=%async_computation.4 | async-start | bytes 131072 | tf_op jit(solution)/shard_map/all_to_all | solution.py:296
  163.6 0.6 copy-start.3

commit v2 on v1

--- a/solution.py
+++ b/solution.py
@@ -57,10 +57,11 @@
 def window_blocks(vectors, more, factors, old):
     n, aux = vectors.shape
     block_d, block_b, _ = factors.shape
-    cons, tail, width = old.shape
-    window = width // block_b
+    cons, own_pairs, count = old.shape
+    window = count // block_d
+    width = window * block_b
+    tail = own_pairs * count // width
     steps = block_d // D_STEP
-    count = window * block_d
 
     def body(v_ref, u_ref, f_ref, p_ref, o_ref, w_ref):
         v = v_ref[...] + u_ref[...]
@@ -90,7 +91,10 @@
                 w = w_ref[h * count : (h + 1) * count].astype(bf16)
                 for j in range(cons):
                     o_ref[j, :count, h * 128 : (h + 1) * 128] = w
-            o_ref[:, count:] = p_ref[...]
+            for j in range(width // count):
+                o_ref[:, count:, j * count : (j + 1) * count] = p_ref[
+                    :, j * tail : (j + 1) * tail, :
+                ]
 
     return pl.pallas_call(
         body,
@@ -108,6 +112,30 @@
     )(vectors, more, factors, old)
 
 
+def old_rows(window_rows, amplitudes):
+    window = window_rows.shape[0]
+    _, block_d, pairs = amplitudes.shape
+
+    def body(*refs):
+        x = jnp.concatenate([r[0].astype(f32) for r in refs[1:-1]], axis=0)
+        refs[-1][...] = x.T.astype(bf16)
+
+    def at(m):
+        return pl.BlockSpec((1, block_d, pairs), lambda i, w: (w[m], 0, 0))
+
+    return pl.pallas_call(
+        body,
+        grid_spec=pltpu.PrefetchScalarGridSpec(
+            num_scalar_prefetch=1,
+            grid=(1,),
+            in_specs=[at(m) for m in range(window)],
+            out_specs=pl.BlockSpec((pairs, window * block_d), lambda i, w: (0, 0)),
+        ),
+        out_shape=jax.ShapeDtypeStruct((pairs, window * block_d), bf16),
+        name="old_rows",
+    )(window_rows, *([amplitudes] * window))
+
+
 def ladder_sums(core, rows, f_own, f_other, t_all, t_other, window):
     count, aux = rows.shape
     block_d, block_b, _ = f_own.shape
@@ -159,7 +187,7 @@
                 pl.BlockSpec((D_STEP, block_b, aux), lambda i, c: (first(i), 0, 0)),
                 pl.BlockSpec((D_STEP, block_b, aux), lambda i, c: (second(i), 0, 0)),
                 pl.BlockSpec((1, D_STEP, c_half, pairs), lambda i, c: (c[0], first(i), 0, 0)),
-                pl.BlockSpec((D_STEP, c_half, pairs), lambda i, c: (second(i), 0, 0)),
+                pl.BlockSpec((1, D_STEP, c_half, pairs), lambda i, c: (c[0], second(i), 0, 0)),
             ],
             out_specs=pl.BlockSpec((pairs, window * block_b), lambda i, c: (0, 0)),
             scratch_shapes=[
@@ -197,17 +225,33 @@
     )(tiles, driver, denom)
 
 
-def second_step(first_all, old, blocks, ladder, driver, denom, window):
+def second_step(first_all, blocks, ladder, driver, denom, window):
     outs, own_pairs, width = first_all.shape
     cons = blocks.shape[0]
     block_b = width // window
     per = cons // outs
     block_d = block_b // per
 
-    def body(f_ref, p_ref, w_ref, l_ref, d_ref, e_ref, o_ref, s_ref):
+    def body(f_ref, w_ref, l_ref, d_ref, e_ref, o_ref, s_ref):
         total = l_ref[...]
+        count = window * block_d
         for o in range(outs):
-            delta = (f_ref[o].astype(f32) - p_ref[o].astype(f32)).astype(bf16)
+            tails = [w_ref[per * o + h, count:, :].astype(f32) for h in range(per)]
+            old = [
+                jnp.concatenate(
+                    [t[:, j * count : (j + 1) * count] for j in range(width // count)], axis=0
+                )
+                for t in tails
+            ]
+            old = jnp.concatenate(
+                [
+                    old[h][:, m * block_d : (m + 1) * block_d]
+                    for m in range(window)
+                    for h in range(per)
+                ],
+                axis=1,
+            )
+            delta = (f_ref[o].astype(f32) - old).astype(bf16)
             for m in range(window):
                 for h in range(per):
                     at = m * block_b + h * block_d
@@ -224,7 +268,7 @@
         out_shape=jax.ShapeDtypeStruct((window, own_pairs, block_b), bf16),
         scratch_shapes=[pltpu.VMEM((width, width), bf16)],
         name="second_step",
-    )(first_all, old, blocks, ladder, driver, denom)
+    )(first_all, blocks, ladder, driver, denom)
 
 
 def update(fitted_factors, amplitudes, driver_term, occ_energy, vir_energy, window_rows):
@@ -253,19 +297,32 @@
     f_other = swap_cores(f_own)
     t_all = amplitudes.reshape(groups, 2, parts, half, block_d, pairs)
     t_all = t_all.transpose(1, 4, 2, 0, 3, 5).reshape(2, block_d, c_half, pairs)
-    t_other = swap_cores(lax.dynamic_index_in_dim(t_all, 1 - core, 0, False))
+    t_other = swap_cores(t_all)
 
     part_i = jnp.arange(parts)[:, None, None]
     group_i = jnp.arange(groups)[None, :, None]
     r_i = jnp.arange(half)[None, None, :]
     c_index = ((group_i * 2 + core) * block_d + part_i * half + r_i).reshape(-1)
 
-    old = jnp.concatenate(
-        [lax.dynamic_slice_in_dim(amplitudes, window_rows[m], 1, 0) for m in range(window)]
+    width = window * block_b
+    old = old_rows(window_rows, amplitudes).reshape(cons, own_pairs, window * block_d)
+
+    rows, f_own, t_all, old = lax.optimization_barrier((rows, f_own, t_all, old))
+
+    at_window = (window_rows[:, None] == c_index[None, :]).astype(bf16)
+    vectors = jnp.einsum(
+        "mc,kcq->kmq", at_window, rows.reshape(window, c_half, aux), preferred_element_type=f32
+    ).astype(bf16)
+    vectors = vectors.reshape(window * window, aux)
+    sent = window_blocks(vectors, swap_cores(vectors), f_own, old)
+    sent, rows = lax.optimization_barrier((sent, rows))
+    got = lax.all_to_all(sent, CON, 0, 0, tiled=True)
+
+    ladder = ladder_sums(core[None], rows, f_own, f_other, t_all, t_other, window)
+    ladder, got, driver_term, occ_energy, vir_energy = lax.optimization_barrier(
+        (ladder, got, driver_term, occ_energy, vir_energy)
     )
-    width = window * block_b
-    old = old.reshape(window, block_d, cons, own_pairs).transpose(2, 3, 0, 1)
-    old = old.reshape(cons, -1, width)
+    tiles = lax.all_to_all(ladder.reshape(cons, own_pairs, width), CON, 0, 0, tiled=True)
 
     mask = window_rows[:, None] == jnp.arange(virtuals, dtype=jnp.int32)[None, :]
     window_energy = jnp.sum(jnp.where(mask, vir_energy[None, :], 0.0), axis=1)
@@ -276,28 +333,10 @@
     driver = lax.dynamic_slice_in_dim(driver_term, con_index * own_pairs, own_pairs, 1)
     driver = driver.transpose(1, 0, 2).reshape(own_pairs, width)
 
-    rows, f_own, f_other, t_all, t_other, old, denom, driver = lax.optimization_barrier(
-        (rows, f_own, f_other, t_all, t_other, old, denom, driver)
-    )
-
-    at_window = (window_rows[:, None] == c_index[None, :]).astype(bf16)
-    vectors = jnp.einsum(
-        "mc,kcq->kmq", at_window, rows.reshape(window, c_half, aux), preferred_element_type=f32
-    ).astype(bf16)
-    vectors = vectors.reshape(window * window, aux)
-    sent = window_blocks(vectors, swap_cores(vectors), f_own, old)
-    sent, rows = lax.optimization_barrier((sent, rows))
-    got = lax.all_to_all(sent, CON, 0, 0, tiled=True)
-
-    ladder = ladder_sums(core[None], rows, f_own, f_other, t_all, t_other, window)
-    ladder, got = lax.optimization_barrier((ladder, got))
-    tiles = lax.all_to_all(ladder.reshape(cons, own_pairs, width), CON, 0, 0, tiled=True)
     ladder_own, first_wide, first_own = first_step(tiles, driver, denom, window, outs)
     first_all = lax.all_to_all(first_wide, OUT, 0, 0, tiled=True)
 
-    old_all = got[:, window * block_d :].reshape(outs, cons // outs, own_pairs, window, block_d)
-    old_all = old_all.transpose(0, 2, 3, 1, 4).reshape(outs, own_pairs, width)
-    second_own = second_step(first_all, old_all, got, ladder_own, driver, denom, window)
+    second_own = second_step(first_all, got, ladder_own, driver, denom, window)
     return (first_own, second_own)
 
 

time: 169 us -> 162 us (0.959)
  waiting for transfers between devices: 28.5 us -> 45.2 us
  local copies, waits for them, and re-layouts: 36.7 us -> 22.3 us
  between operations: 8.28 us -> 0.78 us
  blocking collectives: 30.1 us -> 23.1 us
  starting transfers between devices: 21.5 us -> 25 us
  Pallas kernels: 38.4 us -> 40.6 us
    all_to_all x1, waiting for transfers between devices: 24 us -> 37.4 us  [copy_for_each(): lax.all_to_all(jnp.broadcast_to(value[None], (size, *value.shape)), axis,...]
    all_to_all x1, blocking collectives: 16.1 us -> 9.06 us  [update(): first_all = lax.all_to_all(first_wide, OUT, 0, 0, tiled=True)]
    squeeze x1 -> x0, local copies, waits for them, and re-layouts: 4.59 us -> none  [update(): t_other = swap_cores(lax.dynamic_index_in_dim(t_all, 1 - core, 0, False))]
    all_to_all x1, starting transfers between devices: 3.79 us -> 7.25 us  [update(): lax.all_to_all(ladder.reshape(cons, own_pairs, width), CON, 0, 0, tiled=T...]
    all_to_all x1, waiting for transfers between devices: 3.69 us -> 6.94 us  [update(): lax.all_to_all(ladder.reshape(cons, own_pairs, width), CON, 0, 0, tiled=T...]
    optimization_barrier x1, local copies, waits for them, and re-layouts: 8.95 us -> 6.15 us  [update(): piece, factors = lax.optimization_barrier((piece, fitted_factors))]
    reshape x3 -> x0, local copies, waits for them, and re-layouts: 2.79 us -> none  [the longest x1 1.8 us: update(): old = old.reshape(cons, -1, width)]
    pallas_call x0 -> x1, Pallas kernels: none -> 2.29 us  [old_rows(): pl.pallas_call(body, grid_spec=pltpu.PrefetchScalarGridSpec(num_scalar_pr...]
  transfers between devices with their start and end apart: 6 -> 6, of which waited for: 3 -> 3; matrix products, arithmetic and copies ran while one was open for 17% -> 7% of each run, Pallas kernels for 15% -> 21%
where the time goes in v2:
time: 162 us; the launch traced here: 160 us
  waiting for transfers between devices  45.2 us (28%)
  Pallas kernels  40.6 us (25%)
  starting transfers between devices  25 us (15%)
  blocking collectives  23.1 us (14%)
  local copies, waits for them, and re-layouts  22.3 us (14%)
  other arithmetic  2.42 us (1%)
    all_to_all x1, waiting for transfers between devices, copy_for_each(): lax.all_to_all(jnp.broadcast_to(value[None], (size, *value.shape)), axis,...  37.4 us
    pallas_call x1, Pallas kernels, ladder_sums(): pl.pallas_call(body, grid_spec=pltpu.PrefetchScalarGridSpec(num_scalar_pr...  25.4 us
    all_to_all x1, blocking collectives, update(): lax.all_to_all(owned.reshape(outs, half, aux), OUT, 0, 0, tiled=True)  14 us
    reshape x1, local copies, waits for them, and re-layouts, update(): t_all = amplitudes.reshape(groups, 2, parts, half, block_d, pairs)  11.5 us
    all_to_all x1, starting transfers between devices, copy_for_each(): lax.all_to_all(jnp.broadcast_to(value[None], (size, *value.shape)), axis,...  9.28 us
    all_to_all x1, blocking collectives, update(): first_all = lax.all_to_all(first_wide, OUT, 0, 0, tiled=True)  9.06 us
    all_to_all x1, starting transfers between devices, update(): lax.all_to_all(ladder.reshape(cons, own_pairs, width), CON, 0, 0, tiled=T...  7.25 us
    all_to_all x1, waiting for transfers between devices, update(): lax.all_to_all(ladder.reshape(cons, own_pairs, width), CON, 0, 0, tiled=T...  6.94 us
  transfers between devices with their start and end apart: 6, of which 3 were waited for; matrix products, arithmetic and copies ran while one was open for 7% of the time, Pallas kernels for 21%

profile of v2, /device:TPU:1, one launch (start us, length us, event | category | flops | bytes accessed | tf_op | source)
XLA Modules:
  0.0 159.9 jit_solution(3394374198947982120)
XLA Ops:
  0.6 0.0 copy-start
  0.7 1.2 broadcast_subtract_fusion.1.local_ref
  1.9 2.9 %select_rows.1 = bf16[4,32,1536]{2,1,0:T(8,128)(2,1)} custom-call(s32[4]{0:T(128)} %broadcast_subtract_fusion.1.local_ref, bf16[64,32,1536]{2,1,0:T(8,128)(2,1)} %f_ref.1), custom_call_target="tpu_custom_call" | custom-call | tf_op jit(solution)/shard_map/select_rows/pallas_call | solution.py:44
  4.8 14.0 %all_to_all.25 = bf16[8,16,1536]{2,1,0:T(8,128)(2,1)S(1)} all-to-all(bf16[8,16,1536]{2,1,0:T(8,128)(2,1)} %bitcast.29), channel_id=1, replica_groups=mesh['x'=4,'yl'=2,'z'=4,'yh'=2,'core'=2] {'x','yl'}, dimensions={0} | all-to-all | bytes 786432 | tf_op jit(solution)/shard_map/all_to_all | solution.py:289
  18.8 0.1 reduce_sum.21
  18.8 0.0 slice-start
  18.9 0.0 slice-start.1
  18.9 11.5 %copy.12 = bf16[8,2,2,16,32,256]{5,3,0,2,4,1:T(8,128)(2,1)} copy(bf16[8,2,2,16,32,256]{5,4,3,2,1,0:T(8,128)(2,1)} %bitcast.22) | data formatting | bytes 16777216 | tf_op jit(solution)/shard_map/reshape | solution.py:298
  30.4 2.2 %collective-permute-start.2 = (bf16[2,32,256,256]{3,2,1,0:T(8,128)(2,1)}, bf16[2,32,256,256]{3,2,1,0:T(8,128)(2,1)}, u32[]{:S(2)}, u32[]{:S(2)}) collective-permute-start(bf16[2,32,256,256]{3,2,1,0:T(8,128)(2,1)} %bitcast.27), channel_id=1, source_target_pairs={{0,1},{1,0},{2,3},{3,2},{4,5},{5,4},{6,7},{7,6},{8,9},{9,8},{10,11... | collective-permute-start | bytes 25165832 | tf_op jit(solution)/shard_map/ppermute | solution.py:25
  32.6 0.0 slice-done
  32.6 0.0 slice-done.1
  32.6 6.2 %copy.16 = bf16[64,32,1536]{2,0,1:T(8,128)(2,1)} copy(bf16[64,32,1536]{2,1,0:T(8,128)(2,1)S(1)} %bitcast.24) | data formatting | bytes 12582912 | tf_op jit(solution)/shard_map/optimization_barrier | solution.py:291
  38.7 0.0 collective-permute-start.1
  38.8 2.0 %broadcast_in_dim.13 = bf16[64,16,1536]{2,1,0:T(8,128)(2,1)} broadcast(bf16[16,1536]{1,0:T(8,128)(2,1)S(1)} %reduce_sum.21), dimensions={1,2} | broadcast | bytes 3194880 | tf_op jit(solution)/shard_map/broadcast_in_dim | solution.py:20
  40.8 9.3 %all-to-all-start.1 = ((bf16[64,16,1536]{2,1,0:T(8,128)(2,1)}), bf16[64,16,1536]{2,1,0:T(8,128)(2,1)S(1)}, u32[]{:S(2)}, u32[]{:S(2)}) async-start(bf16[64,16,1536]{2,1,0:T(8,128)(2,1)} %broadcast_in_dim.13), calls=%async_computation.1 | async-start | bytes 6291456 | tf_op jit(solution)/shard_map/all_to_all | solution.py:19
  50.1 0.1 broadcast_add_fusion.2
  50.2 0.1 iota_add_fusion
  50.3 0.1 add.111
  50.3 0.0 copy-start.6
  50.3 2.3 %old_rows.1 = bf16[256,128]{1,0:T(8,128)(2,1)} custom-call(s32[4]{0:T(128)} %refs_0_.1, bf16[512,32,256]{2,1,0:T(8,128)(2,1)} %refs_4_, bf16[512,32,256]{2,1,0:T(8,128)(2,1)} %refs_4_, bf16[512,32,256]{2,1,0:T(8,128)(2,1)} %refs_4_, bf16[512,32,256]{2,1,0:T(8,128)(2,1)} %refs_4_), custom_call_target="tpu_custom_call" | custom-call | tf_op jit(solution)/shard_map/old_rows/pallas_call | solution.py:126
  52.6 37.4 %all-to-all-done.1 = bf16[64,16,1536]{2,1,0:T(8,128)(2,1)S(1)} async-done(((bf16[64,16,1536]{2,1,0:T(8,128)(2,1)}), bf16[64,16,1536]{2,1,0:T(8,128)(2,1)S(1)}, u32[]{:S(2)}, u32[]{:S(2)}) %all-to-all-start.1) | async-done | bytes 3145760 | tf_op jit(solution)/shard_map/all_to_all | solution.py:19
  90.0 0.0 copy-start.1
  90.0 0.0 copy-done.6
  90.0 0.6 fusion
  90.6 0.0 copy-start.4
  90.6 2.4 %collective-permute-start = (bf16[16,1536]{1,0:T(8,128)(2,1)S(1)}, bf16[16,1536]{1,0:T(8,128)(2,1)S(1)}, u32[]{:S(2)}, u32[]{:S(2)}) collective-permute-start(bf16[16,1536]{1,0:T(8,128)(2,1)S(1)} %reshape.124.v_ref), channel_id=1, source_target_pairs={{0,1},{1,0},{2,3},{3,2},{4,5},{5,4},{6,7},{7,6},{8,9},{9,8},{10,11... | collective-permute-start | bytes 147464 | tf_op jit(solution)/shard_map/ppermute | solution.py:25
  93.1 0.9 collective-permute-done.u_ref
  94.0 0.0 copy-done.4
  94.0 0.0 copy-start.5
  94.0 0.6 copy-done.5
  94.6 6.1 %window_blocks.1 = bf16[16,136,256]{2,1,0:T(8,128)(2,1)} custom-call(bf16[16,1536]{1,0:T(8,128)(2,1)} %copy-done.4, bf16[16,1536]{1,0:T(8,128)(2,1)} %copy-done.5, bf16[32,64,1536]{2,1,0:T(8,128)(2,1)} %bitcast.21.f_ref.f1_ref, bf16[16,16,128]{2,1,0:T(8,128)(2,1)} %bitcast.32), custom_call_target="tpu_custom_call" | custom-call | tf_op jit(solution)/shard_map/window_blocks/pallas_call | solution.py:99
  100.6 0.0 copy-done.1
  100.6 3.8 %all-to-all-start.2 = ((bf16[16,136,256]{2,1,0:T(8,128)(2,1)}), bf16[16,136,256]{2,1,0:T(8,128)(2,1)S(1)}, u32[]{:S(2)}, u32[]{:S(2)}) async-start(bf16[16,136,256]{2,1,0:T(8,128)(2,1)} %window_blocks.1), calls=%async_computation.2 | async-start | bytes 2228224 | tf_op jit(solution)/shard_map/all_to_all | solution.py:319
  104.5 0.0 collective-permute-done.1.f2_ref
  104.5 0.0 collective-permute-done.2.t2_ref
  104.5 0.0 copy-start.8
  104.5 0.0 copy-start.7
  104.5 25.4 %ladder_sums.1 = f32[256,256]{1,0:T(8,128)} custom-call(s32[1]{0:T(128)} %bitcast.core_ref, bf16[1024,1536]{1,0:T(8,128)(2,1)} %bitcast.26, bf16[32,64,1536]{2,1,0:T(8,128)(2,1)} %bitcast.21.f_ref.f1_ref, bf16[32,64,1536]{2,1,0:T(8,128)(2,1)} %collective-permute-done.1.f2_ref, bf16[2,32,256,256]{3,2,1,0:T(8,128)(2,1)} %bitcast.28, ...), custom_call_target="tpu_custom_call" | custom-call | flops 15032385536 | bytes 24000000 | tf_op jit(solution)/shard_map/ladder_sums/pallas_call | solution.py:180
  130.0 0.0 all-to-all-done.2.w_ref
  130.0 0.0 copy-done.8
  130.0 0.0 copy-start.2
  130.0 0.2 select_reduce_fusion
  130.2 0.1 dynamic_slice.10
  130.2 0.0 copy-done.7
  130.2 0.1 broadcast_add_fusion
  130.3 7.3 %all-to-all-start.3 = ((f32[16,16,256]{2,1,0:T(8,128)}), f32[16,16,256]{2,1,0:T(8,128)S(1)}, u32[]{:S(2)}, u32[]{:S(2)}) async-start(f32[16,16,256]{2,1,0:T(8,128)} %bitcast.31), calls=%async_computation.3 | async-start | bytes 524288 | tf_op jit(solution)/shard_map/all_to_all | solution.py:325
  137.6 0.1 broadcast_add_fusion.1
  137.6 0.0 copy-done
  137.6 0.1 constant_dynamic-slice_fusion
  137.8 0.1 add.119
  137.8 0.1 add.123
  137.9 0.1 dynamic_slice.11
  138.0 0.7 copy.14.d_ref
  138.7 0.7 broadcast_subtract_fusion.e_ref
  139.3 6.9 %all-to-all-done.3.t_ref = f32[16,16,256]{2,1,0:T(8,128)S(1)} async-done(((f32[16,16,256]{2,1,0:T(8,128)}), f32[16,16,256]{2,1,0:T(8,128)S(1)}, u32[]{:S(2)}, u32[]{:S(2)}) %all-to-all-start.3) | async-done | bytes 262176 | tf_op jit(solution)/shard_map/all_to_all | solution.py:325
  146.3 0.0 copy-start.3
  146.3 0.7 copy-done.3
  147.0 1.7 %first_step.1 = (f32[16,256]{1,0:T(8,128)}, bf16[8,16,256]{2,1,0:T(8,128)(2,1)}, bf16[4,16,64]{2,1,0:T(8,128)(2,1)}) custom-call(f32[16,16,256]{2,1,0:T(8,128)} %copy-done.3, f32[16,256]{1,0:T(8,128)} %copy.14.d_ref, f32[16,256]{1,0:T(8,128)} %broadcast_subtract_fusion.e_ref), custom_call_target="tpu_custom_call" | custom-call | tf_op jit(solution)/shard_map/first_step/pallas_call | solution.py:217
  148.6 9.1 %all_to_all.26.f_ref = bf16[8,16,256]{2,1,0:T(8,128)(2,1)} all-to-all(bf16[8,16,256]{2,1,0:T(8,128)(2,1)} %get-tuple-element.35), channel_id=1, replica_groups=mesh['x'=4,'yl'=2,'z'=4,'yh'=2,'core'=2] {'x','yl'}, dimensions={0} | all-to-all | bytes 131072 | tf_op jit(solution)/shard_map/all_to_all | solution.py:337
  157.7 0.0 copy-done.2
  157.7 2.2 %second_step.1 = bf16[4,16,64]{2,1,0:T(8,128)(2,1)} custom-call(bf16[8,16,256]{2,1,0:T(8,128)(2,1)} %all_to_all.26.f_ref, bf16[16,136,256]{2,1,0:T(8,128)(2,1)} %copy-done.2, f32[16,256]{1,0:T(8,128)} %get-tuple-element.37.l_ref, f32[16,256]{1,0:T(8,128)} %copy.14.d_ref, f32[16,256]{1,0:T(8,128)} %broadcast_subtract_fusion.e_ref), custom_call_target="tpu_custom_call" | custom-call | tf_op jit(solution)/shard_map/second_step/pallas_call | solution.py:266
  (4 shorter events, 0.0 us)
Async XLA Ops:
  0.6 137.0 %copy-start = (f32[4,256,64]{1,2,0:T(8,128)S(1)}, f32[4,256,64]{1,2,0:T(8,128)}, u32[]{:S(2)}) copy-start(f32[4,256,64]{1,2,0:T(8,128)} %param.8) | copy-start | bytes 786436
  18.8 13.7 %slice-start = ((s8[6291456]{0:T(1024)(128)(4,1)}), s8[4194304]{0:T(1024)(128)(4,1)S(1)}, s32[]{:S(2)}) async-start(s8[6291456]{0:T(1024)(128)(4,1)} %bitcast.23), calls=%async_computation.5 | async-start | bytes 8388608
  18.9 13.7 %slice-start.1 = ((s8[6291456]{0:T(1024)(128)(4,1)}), s8[2097152]{0:T(1024)(128)(4,1)S(1)}, s32[]{:S(2)}) async-start(s8[6291456]{0:T(1024)(128)(4,1)} %bitcast.23), calls=%async_computation.6 | async-start | bytes 4194304
  30.4 74.1 %collective-permute-start.2 = (bf16[2,32,256,256]{3,2,1,0:T(8,128)(2,1)}, bf16[2,32,256,256]{3,2,1,0:T(8,128)(2,1)}, u32[]{:S(2)}, u32[]{:S(2)}) collective-permute-start(bf16[2,32,256,256]{3,2,1,0:T(8,128)(2,1)} %bitcast.27), channel_id=1, source_target_pairs={{0,1},{1,0},{2,3},{3,2},{4,5},{5,4},{6,7},{7,6},{8,9},{9,8},{10,11... | collective-permute-start | bytes 25165832 | tf_op jit(solution)/shard_map/ppermute | solution.py:25
  38.7 65.7 %collective-permute-start.1 = (bf16[32,64,1536]{2,1,0:T(8,128)(2,1)}, bf16[32,64,1536]{2,1,0:T(8,128)(2,1)}, u32[]{:S(2)}, u32[]{:S(2)}) collective-permute-start(bf16[32,64,1536]{2,1,0:T(8,128)(2,1)} %bitcast.21.f_ref.f1_ref), channel_id=1, source_target_pairs={{0,1},{1,0},{2,3},{3,2},{4,5},{5,4},{6,7},{7,6},{8,9},{9,8},{10,11... | collective-permute-start | bytes 18874376 | tf_op jit(solution)/shard_map/ppermute | solution.py:25
  40.8 49.2 %all-to-all-start.1 = ((bf16[64,16,1536]{2,1,0:T(8,128)(2,1)}), bf16[64,16,1536]{2,1,0:T(8,128)(2,1)S(1)}, u32[]{:S(2)}, u32[]{:S(2)}) async-start(bf16[64,16,1536]{2,1,0:T(8,128)(2,1)} %broadcast_in_dim.13), calls=%async_computation.1 | async-start | bytes 6291456 | tf_op jit(solution)/shard_map/all_to_all | solution.py:19
  50.3 39.7 %copy-start.6 = (s32[4]{0:T(128)S(1)}, s32[4]{0:T(128)}, u32[]{:S(2)}) copy-start(s32[4]{0:T(128)} %refs_0_.1) | copy-start | bytes 52
  90.0 10.6 %copy-start.1 = (bf16[64,16,1536]{2,1,0:T(8,128)(2,1)}, bf16[64,16,1536]{2,1,0:T(8,128)(2,1)S(1)}, u32[]{:S(2)}) copy-start(bf16[64,16,1536]{2,1,0:T(8,128)(2,1)S(1)} %all-to-all-done.1) | copy-start | bytes 9437188
  90.6 3.3 %copy-start.4 = (bf16[16,1536]{1,0:T(8,128)(2,1)}, bf16[16,1536]{1,0:T(8,128)(2,1)S(1)}, u32[]{:S(2)}) copy-start(bf16[16,1536]{1,0:T(8,128)(2,1)S(1)} %reshape.124.v_ref) | copy-start | bytes 147460
  90.6 3.3 %collective-permute-start = (bf16[16,1536]{1,0:T(8,128)(2,1)S(1)}, bf16[16,1536]{1,0:T(8,128)(2,1)S(1)}, u32[]{:S(2)}, u32[]{:S(2)}) collective-permute-start(bf16[16,1536]{1,0:T(8,128)(2,1)S(1)} %reshape.124.v_ref), channel_id=1, source_target_pairs={{0,1},{1,0},{2,3},{3,2},{4,5},{5,4},{6,7},{7,6},{8,9},{9,8},{10,11... | collective-permute-start | bytes 147464 | tf_op jit(solution)/shard_map/ppermute | solution.py:25
  94.0 0.6 copy-start.5
  100.6 29.3 %all-to-all-start.2 = ((bf16[16,136,256]{2,1,0:T(8,128)(2,1)}), bf16[16,136,256]{2,1,0:T(8,128)(2,1)S(1)}, u32[]{:S(2)}, u32[]{:S(2)}) async-start(bf16[16,136,256]{2,1,0:T(8,128)(2,1)} %window_blocks.1), calls=%async_computation.2 | async-start | bytes 2228224 | tf_op jit(solution)/shard_map/all_to_all | solution.py:319
  104.5 25.5 %copy-start.8 = (f32[512]{0:T(512)S(1)}, f32[512]{0:T(512)}, u32[]{:S(2)}) copy-start(f32[512]{0:T(512)} %param.10) | copy-start | bytes 6148
  104.5 25.7 %copy-start.7 = (f32[16]{0:T(128)S(1)}, f32[16]{0:T(128)}, u32[]{:S(2)}) copy-start(f32[16]{0:T(128)} %param.9) | copy-start | bytes 196
  130.0 27.7 %copy-start.2 = (bf16[16,136,256]{2,1,0:T(8,128)(2,1)}, bf16[16,136,256]{2,1,0:T(8,128)(2,1)S(1)}, u32[]{:S(2)}) copy-start(bf16[16,136,256]{2,1,0:T(8,128)(2,1)S(1)} %all-to-all-done.2.w_ref) | copy-start | bytes 3342340
  130.3 16.0 %all-to-all-start.3 = ((f32[16,16,256]{2,1,0:T(8,128)}), f32[16,16,256]{2,1,0:T(8,128)S(1)}, u32[]{:S(2)}, u32[]{:S(2)}) async-start(f32[16,16,256]{2,1,0:T(8,128)} %bitcast.31), calls=%async_computation.3 | async-start | bytes 524288 | tf_op jit(solution)/shard_map/all_to_all | solution.py:325
  146.3 0.7 copy-start.3

commit v3 on v2

--- a/solution.py
+++ b/solution.py
@@ -29,35 +29,74 @@
     return lax.dot_general(a, b, (((1,), (1,)), ((), ())), preferred_element_type=f32)
 
 
-def select_rows(local, factors):
-    window = local.shape[0]
+def select_rows(window_rows, out_index, factors):
+    window = window_rows.shape[0]
     block_b, block_d, aux = factors.shape
 
-    def body(local_ref, f_ref, o_ref):
-        row = local_ref[pl.program_id(0)]
-        mine = (row >= 0) & (row < block_b)
-        o_ref[...] = jnp.where(mine, f_ref[...], jnp.zeros_like(f_ref))
-
-    def row_map(k, local_ref):
-        return (jnp.clip(local_ref[k], 0, block_b - 1), 0, 0)
-
-    return pl.pallas_call(
-        body,
-        grid_spec=pltpu.PrefetchScalarGridSpec(
-            num_scalar_prefetch=1,
-            grid=(window,),
-            in_specs=[pl.BlockSpec((1, block_d, aux), row_map)],
-            out_specs=pl.BlockSpec((1, block_d, aux), lambda k, _: (k, 0, 0)),
+    def body(w_ref, o_index, *refs):
+        for k in range(window):
+            row = w_ref[k] - o_index[0] * block_b
+            mine = (row >= 0) & (row < block_b)
+            refs[-1][k] = jnp.where(mine, refs[k][0], jnp.zeros_like(refs[k][0]))
+
+    def at(k):
+        def row_map(i, w_ref, o_index):
+            return (jnp.clip(w_ref[k] - o_index[0] * block_b, 0, block_b - 1), 0, 0)
+
+        return pl.BlockSpec((1, block_d, aux), row_map)
+
+    return pl.pallas_call(
+        body,
+        grid_spec=pltpu.PrefetchScalarGridSpec(
+            num_scalar_prefetch=2,
+            grid=(1,),
+            in_specs=[at(k) for k in range(window)],
+            out_specs=pl.BlockSpec((window, block_d, aux), lambda i, w, o: (0, 0, 0)),
         ),
         out_shape=jax.ShapeDtypeStruct((window, block_d, aux), bf16),
         name="select_rows",
-    )(local, factors)
+    )(window_rows, out_index, *([factors] * window))
+
+
+def window_vectors(window_rows, core, rows, block_d):
+    window = window_rows.shape[0]
+    _, _, _, half, aux = rows.shape
+
+    def body(w_ref, c_ref, *refs):
+        for m in range(window):
+            c = w_ref[m]
+            mine = (c // block_d) % 2 == c_ref[0]
+            r = lax.broadcasted_iota(jnp.int32, (half, aux), 0)
+            keep = (r == c % half) & mine
+            for k in range(window):
+                tile = refs[m][k, 0, 0].astype(f32)
+                row = jnp.sum(jnp.where(keep, tile, 0.0), axis=0, keepdims=True)
+                refs[-1][k * window + m : k * window + m + 1, :] = row
+
+    def at(m):
+        def tile_map(i, w_ref, c_ref):
+            c = w_ref[m]
+            return (0, (c % block_d) // half, c // (2 * block_d), 0, 0)
+
+        return pl.BlockSpec((window, 1, 1, half, aux), tile_map)
+
+    return pl.pallas_call(
+        body,
+        grid_spec=pltpu.PrefetchScalarGridSpec(
+            num_scalar_prefetch=2,
+            grid=(1,),
+            in_specs=[at(m) for m in range(window)],
+            out_specs=pl.BlockSpec((window * window, aux), lambda i, w, c: (0, 0)),
+        ),
+        out_shape=jax.ShapeDtypeStruct((window * window, aux), f32),
+        name="window_vectors",
+    )(window_rows, core, *([rows] * window))
 
 
 def window_blocks(vectors, more, factors, old):
     n, aux = vectors.shape
     block_d, block_b, _ = factors.shape
-    cons, own_pairs, count = old.shape
+    chips, cores, own_pairs, count = old.shape
     window = count // block_d
     width = window * block_b
     tail = own_pairs * count // width
@@ -89,12 +128,14 @@
         def _():
             for h in range(width // 128):
                 w = w_ref[h * count : (h + 1) * count].astype(bf16)
-                for j in range(cons):
+                for j in range(chips):
                     o_ref[j, :count, h * 128 : (h + 1) * 128] = w
-            for j in range(width // count):
-                o_ref[:, count:, j * count : (j + 1) * count] = p_ref[
-                    :, j * tail : (j + 1) * tail, :
-                ]
+            for h in range(cores):
+                at = count + h * tail
+                for j in range(width // count):
+                    o_ref[:, at : at + tail, j * count : (j + 1) * count] = p_ref[
+                        :, h, j * tail : (j + 1) * tail, :
+                    ]
 
     return pl.pallas_call(
         body,
@@ -103,10 +144,10 @@
             pl.BlockSpec((n, aux), lambda i: (0, 0)),
             pl.BlockSpec((n, aux), lambda i: (0, 0)),
             pl.BlockSpec((D_STEP, block_b, aux), lambda i: (i, 0, 0)),
-            pl.BlockSpec(old.shape, lambda i: (0, 0, 0)),
+            pl.BlockSpec(old.shape, lambda i: (0, 0, 0, 0)),
         ],
-        out_specs=pl.BlockSpec((cons, count + tail, width), lambda i: (0, 0, 0)),
-        out_shape=jax.ShapeDtypeStruct((cons, count + tail, width), bf16),
+        out_specs=pl.BlockSpec((chips, count + cores * tail, width), lambda i: (0, 0, 0)),
+        out_shape=jax.ShapeDtypeStruct((chips, count + cores * tail, width), bf16),
         scratch_shapes=[pltpu.VMEM((width // 128 * count, 128), f32)],
         name="window_blocks",
     )(vectors, more, factors, old)
@@ -225,50 +266,61 @@
     )(tiles, driver, denom)
 
 
-def second_step(first_all, blocks, ladder, driver, denom, window):
+def second_step(core, first_all, blocks, other, ladder, driver, denom, window):
     outs, own_pairs, width = first_all.shape
-    cons = blocks.shape[0]
     block_b = width // window
-    per = cons // outs
-    block_d = block_b // per
-
-    def body(f_ref, w_ref, l_ref, d_ref, e_ref, o_ref, s_ref):
+    block_d = block_b // 2
+    count = window * block_d
+    tail = own_pairs * count // width
+
+    def body(c_ref, f_ref, w_ref, x_ref, l_ref, d_ref, e_ref, o_ref, s_ref):
         total = l_ref[...]
-        count = window * block_d
+        south = c_ref[0] == 0
         for o in range(outs):
-            tails = [w_ref[per * o + h, count:, :].astype(f32) for h in range(per)]
-            old = [
-                jnp.concatenate(
-                    [t[:, j * count : (j + 1) * count] for j in range(width // count)], axis=0
+            mine, theirs = w_ref[o, :count, :], x_ref[o, :count, :]
+            halves = (jnp.where(south, mine, theirs), jnp.where(south, theirs, mine))
+            olds = []
+            for ref in (w_ref, x_ref):
+                t = jnp.where(
+                    south, ref[o, count : count + tail, :], ref[o, count + tail :, :]
+                ).astype(f32)
+                olds.append(
+                    jnp.concatenate(
+                        [t[:, j * count : (j + 1) * count] for j in range(width // count)], axis=0
+                    )
                 )
-                for t in tails
-            ]
+            olds = (jnp.where(south, olds[0], olds[1]), jnp.where(south, olds[1], olds[0]))
             old = jnp.concatenate(
                 [
-                    old[h][:, m * block_d : (m + 1) * block_d]
+                    olds[h][:, m * block_d : (m + 1) * block_d]
                     for m in range(window)
-                    for h in range(per)
+                    for h in range(2)
                 ],
                 axis=1,
             )
             delta = (f_ref[o].astype(f32) - old).astype(bf16)
             for m in range(window):
-                for h in range(per):
+                for h in range(2):
                     at = m * block_b + h * block_d
-                    s_ref[at : at + block_d, :] = w_ref[
-                        per * o + h, m * block_d : (m + 1) * block_d, :
-                    ]
+                    s_ref[at : at + block_d, :] = halves[h][m * block_d : (m + 1) * block_d, :]
             total = total + jnp.dot(delta, s_ref[...], preferred_element_type=f32)
         value = ((d_ref[...] + total) / e_ref[...]).astype(bf16)
         for k in range(window):
             o_ref[k] = value[:, k * block_b : (k + 1) * block_b]
 
-    return pl.pallas_call(
-        body,
+    whole = [first_all, blocks, other, ladder, driver, denom]
+    return pl.pallas_call(
+        body,
+        grid_spec=pltpu.PrefetchScalarGridSpec(
+            num_scalar_prefetch=1,
+            grid=(1,),
+            in_specs=[pl.BlockSpec(x.shape, lambda i, c, n=x.ndim: (0,) * n) for x in whole],
+            out_specs=pl.BlockSpec((window, own_pairs, block_b), lambda i, c: (0, 0, 0)),
+            scratch_shapes=[pltpu.VMEM((width, width), bf16)],
+        ),
         out_shape=jax.ShapeDtypeStruct((window, own_pairs, block_b), bf16),
-        scratch_shapes=[pltpu.VMEM((width, width), bf16)],
         name="second_step",
-    )(first_all, blocks, ladder, driver, denom)
+    )(core, *whole)
 
 
 def update(fitted_factors, amplitudes, driver_term, occ_energy, vir_energy, window_rows):
@@ -285,7 +337,7 @@
     c_half = parts * groups * half
     own_pairs = pairs // cons
 
-    owned = select_rows(window_rows - out_index.astype(jnp.int32) * block_b, fitted_factors)
+    owned = select_rows(window_rows, out_index.astype(jnp.int32)[None], fitted_factors)
     tiles = lax.all_to_all(owned.reshape(outs, half, aux), OUT, 0, 0, tiled=True)
     piece = jnp.sum(tiles.astype(f32), axis=0).astype(bf16)
     piece, factors = lax.optimization_barrier((piece, fitted_factors))
@@ -299,24 +351,17 @@
     t_all = t_all.transpose(1, 4, 2, 0, 3, 5).reshape(2, block_d, c_half, pairs)
     t_other = swap_cores(t_all)
 
-    part_i = jnp.arange(parts)[:, None, None]
-    group_i = jnp.arange(groups)[None, :, None]
-    r_i = jnp.arange(half)[None, None, :]
-    c_index = ((group_i * 2 + core) * block_d + part_i * half + r_i).reshape(-1)
-
     width = window * block_b
-    old = old_rows(window_rows, amplitudes).reshape(cons, own_pairs, window * block_d)
+    old = old_rows(window_rows, amplitudes).reshape(groups, 2, own_pairs, window * block_d)
 
     rows, f_own, t_all, old = lax.optimization_barrier((rows, f_own, t_all, old))
 
-    at_window = (window_rows[:, None] == c_index[None, :]).astype(bf16)
-    vectors = jnp.einsum(
-        "mc,kcq->kmq", at_window, rows.reshape(window, c_half, aux), preferred_element_type=f32
+    vectors = window_vectors(
+        window_rows, core[None], rows.reshape(window, parts, groups, half, aux), block_d
     ).astype(bf16)
-    vectors = vectors.reshape(window * window, aux)
     sent = window_blocks(vectors, swap_cores(vectors), f_own, old)
     sent, rows = lax.optimization_barrier((sent, rows))
-    got = lax.all_to_all(sent, CON, 0, 0, tiled=True)
+    got = lax.all_to_all(sent, CON[:-1], 0, 0, tiled=True)
 
     ladder = ladder_sums(core[None], rows, f_own, f_other, t_all, t_other, window)
     ladder, got, driver_term, occ_energy, vir_energy = lax.optimization_barrier(
@@ -336,7 +381,9 @@
     ladder_own, first_wide, first_own = first_step(tiles, driver, denom, window, outs)
     first_all = lax.all_to_all(first_wide, OUT, 0, 0, tiled=True)
 
-    second_own = second_step(first_all, got, ladder_own, driver, denom, window)
+    second_own = second_step(
+        core[None], first_all, got, swap_cores(got), ladder_own, driver, denom, window
+    )
     return (first_own, second_own)
 
 

time: 162 us -> 165 us (1.019)
  local copies, waits for them, and re-layouts: 22.3 us -> 24.7 us
  Pallas kernels: 40.6 us -> 42.9 us
    pallas_call x1 -> x2, Pallas kernels: 2.23 us -> 5.15 us  [the longest x1 2.89 us: window_vectors(): pl.pallas_call(body, grid_spec=pltpu.PrefetchScalarGridSpec(num_scalar_pr...]
    unnamed x22 -> x24, local copies, waits for them, and re-layouts: 1.36 us -> 3.83 us
    ppermute x3 -> x4, starting transfers between devices: 4.62 us -> 4.8 us  [swap_cores(): return lax.ppermute(value, 'core', [(0, 1), (1, 0)])]
  transfers between devices with their start and end apart: 6 -> 7, of which waited for: 3 -> 3; matrix products, arithmetic and copies ran while one was open for 7% -> 7% of each run, Pallas kernels for 21% -> 23%
where the time goes in v3:
time: 165 us; the launch traced here: 163 us
  waiting for transfers between devices  45.4 us (28%)
  Pallas kernels  42.9 us (26%)
  starting transfers between devices  25.1 us (15%)
  local copies, waits for them, and re-layouts  24.7 us (15%)
  blocking collectives  22.1 us (13%)
  other arithmetic  1.95 us (1%)
    all_to_all x1, waiting for transfers between devices, copy_for_each(): lax.all_to_all(jnp.broadcast_to(value[None], (size, *value.shape)), axis,...  37.8 us
    pallas_call x1, Pallas kernels, ladder_sums(): pl.pallas_call(body, grid_spec=pltpu.PrefetchScalarGridSpec(num_scalar_pr...  25.4 us
    all_to_all x1, blocking collectives, update(): lax.all_to_all(owned.reshape(outs, half, aux), OUT, 0, 0, tiled=True)  13.1 us
    reshape x1, local copies, waits for them, and re-layouts, update(): t_all = amplitudes.reshape(groups, 2, parts, half, block_d, pairs)  11.6 us
    all_to_all x1, starting transfers between devices, copy_for_each(): lax.all_to_all(jnp.broadcast_to(value[None], (size, *value.shape)), axis,...  9.28 us
    all_to_all x1, blocking collectives, update(): first_all = lax.all_to_all(first_wide, OUT, 0, 0, tiled=True)  9.06 us
    all_to_all x1, starting transfers between devices, update(): lax.all_to_all(ladder.reshape(cons, own_pairs, width), CON, 0, 0, tiled=T...  7.46 us
    all_to_all x1, waiting for transfers between devices, update(): lax.all_to_all(ladder.reshape(cons, own_pairs, width), CON, 0, 0, tiled=T...  6.76 us
  transfers between devices with their start and end apart: 7, of which 3 were waited for; matrix products, arithmetic and copies ran while one was open for 7% of the time, Pallas kernels for 23%

profile of v3, /device:TPU:1, one launch (start us, length us, event | category | flops | bytes accessed | tf_op | source)
XLA Modules:
  0.0 162.9 jit_solution(17886418839326918900)
XLA Ops:
  0.6 0.0 copy-start
  0.7 2.7 %select_rows.1 = bf16[4,32,1536]{2,1,0:T(8,128)(2,1)} custom-call(s32[4]{0:T(128)} %w_ref.3, s32[1]{0:T(128)} %bitcast.1.o_index, bf16[64,32,1536]{2,1,0:T(8,128)(2,1)} %refs_3_.1, bf16[64,32,1536]{2,1,0:T(8,128)(2,1)} %refs_3_.1, bf16[64,32,1536]{2,1,0:T(8,128)(2,1)} %refs_3_.1, bf16[64,32,1536]{2,1,0:T(8,128)(2,1)} %refs_3_.1), custom_call_target="tpu_custom_call" | custom-call | tf_op jit(solution)/shard_map/select_rows/pallas_call | solution.py:48
  3.3 13.1 %all_to_all.25 = bf16[8,16,1536]{2,1,0:T(8,128)(2,1)S(1)} all-to-all(bf16[8,16,1536]{2,1,0:T(8,128)(2,1)} %bitcast.27), channel_id=1, replica_groups=mesh['x'=4,'yl'=2,'z'=4,'yh'=2,'core'=2] {'x','yl'}, dimensions={0} | all-to-all | bytes 786432 | tf_op jit(solution)/shard_map/all_to_all | solution.py:341
  16.4 0.0 slice-start
  16.4 0.1 reduce_sum.21
  16.5 0.0 slice-start.1
  16.5 11.6 %copy.12 = bf16[8,2,2,16,32,256]{5,3,0,2,4,1:T(8,128)(2,1)} copy(bf16[8,2,2,16,32,256]{5,4,3,2,1,0:T(8,128)(2,1)} %bitcast.17) | data formatting | bytes 16777216 | tf_op jit(solution)/shard_map/reshape | solution.py:350
  28.0 2.2 %collective-permute-start.2 = (bf16[2,32,256,256]{3,2,1,0:T(8,128)(2,1)}, bf16[2,32,256,256]{3,2,1,0:T(8,128)(2,1)}, u32[]{:S(2)}, u32[]{:S(2)}) collective-permute-start(bf16[2,32,256,256]{3,2,1,0:T(8,128)(2,1)} %bitcast.25), channel_id=1, source_target_pairs={{0,1},{1,0},{2,3},{3,2},{4,5},{5,4},{6,7},{7,6},{8,9},{9,8},{10,11... | collective-permute-start | bytes 25165832 | tf_op jit(solution)/shard_map/ppermute | solution.py:25
  30.2 0.0 slice-done
  30.2 0.0 slice-done.1
  30.2 6.2 %copy.16 = bf16[64,32,1536]{2,0,1:T(8,128)(2,1)} copy(bf16[64,32,1536]{2,1,0:T(8,128)(2,1)S(1)} %bitcast.19) | data formatting | bytes 12582912 | tf_op jit(solution)/shard_map/optimization_barrier | solution.py:343
  36.4 0.0 collective-permute-start.1
  36.4 2.0 %broadcast_in_dim.20 = bf16[64,16,1536]{2,1,0:T(8,128)(2,1)} broadcast(bf16[16,1536]{1,0:T(8,128)(2,1)S(1)} %reduce_sum.21), dimensions={1,2} | broadcast | bytes 3194880 | tf_op jit(solution)/shard_map/broadcast_in_dim | solution.py:20
  38.4 9.3 %all-to-all-start.1 = ((bf16[64,16,1536]{2,1,0:T(8,128)(2,1)}), bf16[64,16,1536]{2,1,0:T(8,128)(2,1)S(1)}, u32[]{:S(2)}, u32[]{:S(2)}) async-start(bf16[64,16,1536]{2,1,0:T(8,128)(2,1)} %broadcast_in_dim.20), calls=%async_computation.1 | async-start | bytes 6291456 | tf_op jit(solution)/shard_map/all_to_all | solution.py:19
  47.7 2.2 %old_rows.1 = bf16[256,128]{1,0:T(8,128)(2,1)} custom-call(s32[4]{0:T(128)} %w_ref.3, bf16[512,32,256]{2,1,0:T(8,128)(2,1)} %refs_4_, bf16[512,32,256]{2,1,0:T(8,128)(2,1)} %refs_4_, bf16[512,32,256]{2,1,0:T(8,128)(2,1)} %refs_4_, bf16[512,32,256]{2,1,0:T(8,128)(2,1)} %refs_4_), custom_call_target="tpu_custom_call" | custom-call | tf_op jit(solution)/shard_map/old_rows/pallas_call | solution.py:167
  49.9 37.8 %all-to-all-done.1 = bf16[64,16,1536]{2,1,0:T(8,128)(2,1)S(1)} async-done(((bf16[64,16,1536]{2,1,0:T(8,128)(2,1)}), bf16[64,16,1536]{2,1,0:T(8,128)(2,1)S(1)}, u32[]{:S(2)}, u32[]{:S(2)}) %all-to-all-start.1) | async-done | bytes 3145760 | tf_op jit(solution)/shard_map/all_to_all | solution.py:19
  87.7 0.0 copy-start.1
  87.7 1.7 %copy-done.1 = bf16[64,16,1536]{2,1,0:T(8,128)(2,1)} copy-done((bf16[64,16,1536]{2,1,0:T(8,128)(2,1)}, bf16[64,16,1536]{2,1,0:T(8,128)(2,1)S(1)}, u32[]{:S(2)}) %copy-start.1) | copy-done | bytes 3145752
  89.3 2.9 %window_vectors.1 = f32[16,1536]{1,0:T(8,128)} custom-call(s32[4]{0:T(128)} %w_ref.3, s32[1]{0:T(128)} %bitcast.c_ref.core_ref, bf16[4,2,8,16,1536]{4,3,2,1,0:T(8,128)(2,1)} %bitcast.20, bf16[4,2,8,16,1536]{4,3,2,1,0:T(8,128)(2,1)} %bitcast.21, bf16[4,2,8,16,1536]{4,3,2,1,0:T(8,128)(2,1)} %bitcast.22, bf16[4,2,8,16,1536]{4,3,2,1,0:T(8,128)(2,1)} %bitcast.23), custom_call_target="tpu_custom_call" | custom-call | tf_op jit(solution)/shard_map/window_vectors/pallas_call | solution.py:83
  92.2 0.9 convert_element_type.2.v_ref
  93.1 0.0 copy-start.5
  93.1 2.4 %collective-permute-start = (bf16[16,1536]{1,0:T(8,128)(2,1)S(1)}, bf16[16,1536]{1,0:T(8,128)(2,1)S(1)}, u32[]{:S(2)}, u32[]{:S(2)}) collective-permute-start(bf16[16,1536]{1,0:T(8,128)(2,1)S(1)} %convert_element_type.2.v_ref), channel_id=1, source_target_pairs={{0,1},{1,0},{2,3},{3,2},{4,5},{5,4},{6,7},{7,6},{8,9},{9,8},{10,11... | collective-permute-start | bytes 147464 | tf_op jit(solution)/shard_map/ppermute | solution.py:25
  95.5 0.9 collective-permute-done.u_ref
  96.4 0.0 copy-done.5
  96.4 0.0 copy-start.6
  96.4 0.6 copy-done.6
  97.0 5.8 %window_blocks.1 = bf16[8,144,256]{2,1,0:T(8,128)(2,1)} custom-call(bf16[16,1536]{1,0:T(8,128)(2,1)} %copy-done.5, bf16[16,1536]{1,0:T(8,128)(2,1)} %copy-done.6, bf16[32,64,1536]{2,1,0:T(8,128)(2,1)} %bitcast.16.f_ref.f1_ref, bf16[8,2,16,128]{3,2,1,0:T(8,128)(2,1)} %bitcast.29), custom_call_target="tpu_custom_call" | custom-call | tf_op jit(solution)/shard_map/window_blocks/pallas_call | solution.py:140
  102.9 3.5 %all-to-all-start.2 = ((bf16[8,144,256]{2,1,0:T(8,128)(2,1)}), bf16[8,144,256]{2,1,0:T(8,128)(2,1)S(1)}, u32[]{:S(2)}, u32[]{:S(2)}) async-start(bf16[8,144,256]{2,1,0:T(8,128)(2,1)} %window_blocks.1), calls=%async_computation.2 | async-start | bytes 1179648 | tf_op jit(solution)/shard_map/all_to_all | solution.py:364
  106.4 0.0 copy-start.7
  106.4 0.0 copy-start.9
  106.4 0.0 copy-start.8
  106.5 0.0 collective-permute-done.1.f2_ref
  106.5 0.0 collective-permute-done.2.t2_ref
  106.5 25.4 %ladder_sums.1 = f32[256,256]{1,0:T(8,128)} custom-call(s32[1]{0:T(128)} %bitcast.c_ref.core_ref, bf16[1024,1536]{1,0:T(8,128)(2,1)} %bitcast.24, bf16[32,64,1536]{2,1,0:T(8,128)(2,1)} %bitcast.16.f_ref.f1_ref, bf16[32,64,1536]{2,1,0:T(8,128)(2,1)} %collective-permute-done.1.f2_ref, bf16[2,32,256,256]{3,2,1,0:T(8,128)(2,1)} %bitcast.26, ...), custom_call_target="tpu_custom_call" | custom-call | flops 15032385536 | bytes 24000000 | tf_op jit(solution)/shard_map/ladder_sums/pallas_call | solution.py:221
  131.9 0.0 all-to-all-done.2.w_ref
  131.9 0.0 copy-done.7
  131.9 0.0 copy-done.9
  131.9 0.0 copy-start.2
  131.9 0.2 select_reduce_fusion
  132.1 0.1 dynamic_slice.10
  132.2 0.0 copy-done.8
  132.2 0.1 broadcast_add_fusion
  132.3 7.5 %all-to-all-start.3 = ((f32[16,16,256]{2,1,0:T(8,128)}), f32[16,16,256]{2,1,0:T(8,128)S(1)}, u32[]{:S(2)}, u32[]{:S(2)}) async-start(f32[16,16,256]{2,1,0:T(8,128)} %bitcast.30), calls=%async_computation.3 | async-start | bytes 524288 | tf_op jit(solution)/shard_map/all_to_all | solution.py:370
  139.7 0.2 collective-permute-start.3
  139.9 0.1 broadcast_add_fusion.1
  140.0 0.0 copy-done
  140.0 0.1 constant_dynamic-slice_fusion
  140.1 0.1 add.61
  140.2 0.1 add.65
  140.2 0.1 dynamic_slice.11
  140.3 0.7 copy.14.d_ref
  141.0 0.7 broadcast_subtract_fusion.e_ref
  141.7 6.8 %all-to-all-done.3.t_ref = f32[16,16,256]{2,1,0:T(8,128)S(1)} async-done(((f32[16,16,256]{2,1,0:T(8,128)}), f32[16,16,256]{2,1,0:T(8,128)S(1)}, u32[]{:S(2)}, u32[]{:S(2)}) %all-to-all-start.3) | async-done | bytes 262176 | tf_op jit(solution)/shard_map/all_to_all | solution.py:370
  148.4 0.0 copy-start.3
  148.4 0.7 copy-done.3
  149.1 1.7 %first_step.1 = (f32[16,256]{1,0:T(8,128)}, bf16[8,16,256]{2,1,0:T(8,128)(2,1)}, bf16[4,16,64]{2,1,0:T(8,128)(2,1)}) custom-call(f32[16,16,256]{2,1,0:T(8,128)} %copy-done.3, f32[16,256]{1,0:T(8,128)} %copy.14.d_ref, f32[16,256]{1,0:T(8,128)} %broadcast_subtract_fusion.e_ref), custom_call_target="tpu_custom_call" | custom-call | tf_op jit(solution)/shard_map/first_step/pallas_call | solution.py:258
  150.8 9.1 %all_to_all.26.f_ref = bf16[8,16,256]{2,1,0:T(8,128)(2,1)} all-to-all(bf16[8,16,256]{2,1,0:T(8,128)(2,1)} %get-tuple-element.35), channel_id=1, replica_groups=mesh['x'=4,'yl'=2,'z'=4,'yh'=2,'core'=2] {'x','yl'}, dimensions={0} | all-to-all | bytes 131072 | tf_op jit(solution)/shard_map/all_to_all | solution.py:382
  159.8 0.0 collective-permute-done.3.x_ref
  159.8 0.0 copy-start.4
  159.8 0.0 copy-done.2
  159.9 0.8 copy-done.4
  160.7 2.3 %second_step.1 = bf16[4,16,64]{2,1,0:T(8,128)(2,1)} custom-call(s32[1]{0:T(128)} %bitcast.c_ref.core_ref, bf16[8,16,256]{2,1,0:T(8,128)(2,1)} %all_to_all.26.f_ref, bf16[8,144,256]{2,1,0:T(8,128)(2,1)} %copy-done.2, bf16[8,144,256]{2,1,0:T(8,128)(2,1)} %copy-done.4, f32[16,256]{1,0:T(8,128)} %get-tuple-element.37.l_ref, f32[16,256]{1,0:T(8,128)} %copy.14.d_ref, ...), custom_call_target="tpu_custom_call" | custom-call | tf_op jit(solution)/shard_map/second_step/pallas_call | solution.py:312
  (1 shorter events, 0.0 us)
Async XLA Ops:
  0.6 139.3 %copy-start = (f32[4,256,64]{1,2,0:T(8,128)S(1)}, f32[4,256,64]{1,2,0:T(8,128)}, u32[]{:S(2)}) copy-start(f32[4,256,64]{1,2,0:T(8,128)} %param.8) | copy-start | bytes 786436
  16.4 13.8 %slice-start = ((s8[6291456]{0:T(1024)(128)(4,1)}), s8[2097152]{0:T(1024)(128)(4,1)S(1)}, s32[]{:S(2)}) async-start(s8[6291456]{0:T(1024)(128)(4,1)} %bitcast.18), calls=%async_computation.5 | async-start | bytes 4194304
  16.5 13.7 %slice-start.1 = ((s8[6291456]{0:T(1024)(128)(4,1)}), s8[4194304]{0:T(1024)(128)(4,1)S(1)}, s32[]{:S(2)}) async-start(s8[6291456]{0:T(1024)(128)(4,1)} %bitcast.18), calls=%async_computation.6 | async-start | bytes 8388608
  28.0 78.4 %collective-permute-start.2 = (bf16[2,32,256,256]{3,2,1,0:T(8,128)(2,1)}, bf16[2,32,256,256]{3,2,1,0:T(8,128)(2,1)}, u32[]{:S(2)}, u32[]{:S(2)}) collective-permute-start(bf16[2,32,256,256]{3,2,1,0:T(8,128)(2,1)} %bitcast.25), channel_id=1, source_target_pairs={{0,1},{1,0},{2,3},{3,2},{4,5},{5,4},{6,7},{7,6},{8,9},{9,8},{10,11... | collective-permute-start | bytes 25165832 | tf_op jit(solution)/shard_map/ppermute | solution.py:25
  36.4 70.1 %collective-permute-start.1 = (bf16[32,64,1536]{2,1,0:T(8,128)(2,1)}, bf16[32,64,1536]{2,1,0:T(8,128)(2,1)}, u32[]{:S(2)}, u32[]{:S(2)}) collective-permute-start(bf16[32,64,1536]{2,1,0:T(8,128)(2,1)} %bitcast.16.f_ref.f1_ref), channel_id=1, source_target_pairs={{0,1},{1,0},{2,3},{3,2},{4,5},{5,4},{6,7},{7,6},{8,9},{9,8},{10,11... | collective-permute-start | bytes 18874376 | tf_op jit(solution)/shard_map/ppermute | solution.py:25
  38.4 49.2 %all-to-all-start.1 = ((bf16[64,16,1536]{2,1,0:T(8,128)(2,1)}), bf16[64,16,1536]{2,1,0:T(8,128)(2,1)S(1)}, u32[]{:S(2)}, u32[]{:S(2)}) async-start(bf16[64,16,1536]{2,1,0:T(8,128)(2,1)} %broadcast_in_dim.20), calls=%async_computation.1 | async-start | bytes 6291456 | tf_op jit(solution)/shard_map/all_to_all | solution.py:19
  87.7 1.7 %copy-start.1 = (bf16[64,16,1536]{2,1,0:T(8,128)(2,1)}, bf16[64,16,1536]{2,1,0:T(8,128)(2,1)S(1)}, u32[]{:S(2)}) copy-start(bf16[64,16,1536]{2,1,0:T(8,128)(2,1)S(1)} %all-to-all-done.1) | copy-start | bytes 9437188
  93.1 3.3 %copy-start.5 = (bf16[16,1536]{1,0:T(8,128)(2,1)}, bf16[16,1536]{1,0:T(8,128)(2,1)S(1)}, u32[]{:S(2)}) copy-start(bf16[16,1536]{1,0:T(8,128)(2,1)S(1)} %convert_element_type.2.v_ref) | copy-start | bytes 147460
  93.1 3.3 %collective-permute-start = (bf16[16,1536]{1,0:T(8,128)(2,1)S(1)}, bf16[16,1536]{1,0:T(8,128)(2,1)S(1)}, u32[]{:S(2)}, u32[]{:S(2)}) collective-permute-start(bf16[16,1536]{1,0:T(8,128)(2,1)S(1)} %convert_element_type.2.v_ref), channel_id=1, source_target_pairs={{0,1},{1,0},{2,3},{3,2},{4,5},{5,4},{6,7},{7,6},{8,9},{9,8},{10,11... | collective-permute-start | bytes 147464 | tf_op jit(solution)/shard_map/ppermute | solution.py:25
  96.4 0.6 copy-start.6
  102.9 29.0 %all-to-all-start.2 = ((bf16[8,144,256]{2,1,0:T(8,128)(2,1)}), bf16[8,144,256]{2,1,0:T(8,128)(2,1)S(1)}, u32[]{:S(2)}, u32[]{:S(2)}) async-start(bf16[8,144,256]{2,1,0:T(8,128)(2,1)} %window_blocks.1), calls=%async_computation.2 | async-start | bytes 1179648 | tf_op jit(solution)/shard_map/all_to_all | solution.py:364
  106.4 25.5 %copy-start.7 = (s32[4]{0:T(128)S(1)}, s32[4]{0:T(128)}, u32[]{:S(2)}) copy-start(s32[4]{0:T(128)} %w_ref.3) | copy-start | bytes 52
  106.4 25.5 %copy-start.9 = (f32[512]{0:T(512)S(1)}, f32[512]{0:T(512)}, u32[]{:S(2)}) copy-start(f32[512]{0:T(512)} %param.10) | copy-start | bytes 6148
  106.4 25.7 %copy-start.8 = (f32[16]{0:T(128)S(1)}, f32[16]{0:T(128)}, u32[]{:S(2)}) copy-start(f32[16]{0:T(128)} %param.9) | copy-start | bytes 196
  131.9 27.9 %copy-start.2 = (bf16[8,144,256]{2,1,0:T(8,128)(2,1)}, bf16[8,144,256]{2,1,0:T(8,128)(2,1)S(1)}, u32[]{:S(2)}) copy-start(bf16[8,144,256]{2,1,0:T(8,128)(2,1)S(1)} %all-to-all-done.2.w_ref) | copy-start | bytes 1769476
  132.3 16.2 %all-to-all-start.3 = ((f32[16,16,256]{2,1,0:T(8,128)}), f32[16,16,256]{2,1,0:T(8,128)S(1)}, u32[]{:S(2)}, u32[]{:S(2)}) async-start(f32[16,16,256]{2,1,0:T(8,128)} %bitcast.30), calls=%async_computation.3 | async-start | bytes 524288 | tf_op jit(solution)/shard_map/all_to_all | solution.py:370
  139.7 20.1 %collective-permute-start.3 = (bf16[8,144,256]{2,1,0:T(8,128)(2,1)S(1)}, bf16[8,144,256]{2,1,0:T(8,128)(2,1)S(1)}, u32[]{:S(2)}, u32[]{:S(2)}) collective-permute-start(bf16[8,144,256]{2,1,0:T(8,128)(2,1)S(1)} %all-to-all-done.2.w_ref), channel_id=1, source_target_pairs={{0,1},{1,0},{2,3},{3,2},{4,5},{5,4},{6,7},{7,6},{8,9},{9,8},{10,11... | collective-permute-start | bytes 1769480 | tf_op jit(solution)/shard_map/ppermute | solution.py:25
  148.4 0.7 copy-start.3
  159.8 0.8 copy-start.4
